TPU v7x, 512 devices: a whole 4x4x16 slice. The times are simulated.
512 devices in a mesh: group: 16 (over z), row: 8 (over x, core), col: 4 (over y).
Axes of the slice: x: 4, y: 4, z: 16, core: 2. Of those that a mesh axis runs over, the one named last changes fastest.
Arguments:
- child_front: float32 [16, 4, 4, 128, 2, 8, 128], P('group', None, 'col', None, None, 'row'), as said below
- top_front: float32 [12, 4, 16, 8, 6, 8, 128], P(None, 'col', 'group', None, None, 'row'), as said below
- block_map: int32 [16, 8], replicated, may hold values from 0 to 47, as said below
- pivots: int32 [16], P('group'), may hold values from 512 to 1024, as said below
- noise: float32 [16, 1024], P('group'), may hold values from -6 to 6
- top_sample: float32 [6144], replicated, may hold values from -12 to 12
Outputs:
- top_out: float32 [12, 4, 16, 8, 6, 8, 128], P(None, 'col', 'group', None, None, 'row')
- child_sample: float32 [16, 1024], P('group')
Inputs may be any that keep to these rules, and one draw needn't show every extreme that they name: `child_front`: each child front is symmetric positive definite. `top_front`: symmetric positive definite. block_map[g, u] mod 8 equals u; the entries of one row are distinct. `pivots`: A multiple of 128; some child has 1024.
All inputs are finite; a program needn't handle non-finite values.
Results may differ from a plain program's by a relative error of at most 0.00015.
Values sent between devices are 32-bit elements; how exact they have to be, the bound alone decides.
No kernel may reach another device: no remote copies, remote signals or barrier semaphores. Data moves between devices by JAX's collectives and lax.ppermute only.
A program may use at most 64 MiB of HBM per device.

v0:
```python
import math

import jax
import jax.numpy as jnp
from jax import lax
from jax.sharding import PartitionSpec as P

HIGH = lax.Precision.HIGHEST


def laid_out(parts, dim):
    dims = list(parts.shape[1:])
    dims[dim] *= parts.shape[0]
    return jnp.moveaxis(parts, 0, dim).reshape(dims)


def from_everyone(value, axis):
    copies = jnp.broadcast_to(value, (lax.axis_size(axis), *value.shape))
    return lax.all_to_all(copies, axis, split_axis=0, concat_axis=0, tiled=True)


def gather_directly(value, axis, dim):
    return laid_out(from_everyone(value, axis), dim)


def from_root(value, axis, root):
    return lax.dynamic_index_in_dim(lax.all_gather(value, axis), root, 0, keepdims=False)


def taken_together(value, axis):
    return from_everyone(value, axis).sum(axis=0)


def cross_product(left_side, right_side):
    return lax.dot_general(left_side, right_side, (((0,), (0,)), ((), ())), precision=HIGH)


def global_index(local_blocks, stride, position, block_rows):
    starts = jnp.arange(local_blocks, dtype=jnp.int32)[:, None] * stride + position
    return (starts * block_rows + jnp.arange(block_rows, dtype=jnp.int32)[None, :]).reshape(-1)


def diagonal_from_rows(gathered, panel_index, first_block, row_count, col_count, block_rows):
    panel_width = gathered.shape[0]
    span_blocks = gathered.shape[2] // block_rows
    ordered = gathered.reshape(panel_width, row_count, span_blocks, block_rows)
    ordered = ordered.transpose(0, 2, 1, 3).reshape(
        panel_width, span_blocks * row_count * block_rows
    )
    offset = (panel_index * col_count - first_block * row_count) * block_rows
    return ordered[:, offset : offset + panel_width]


def pick_columns(received, local_blocks, my_col, row_count, col_count):
    pieces = []
    for local_block in range(local_blocks):
        global_block = local_block * col_count + my_col
        source = received[local_block % len(received)]
        pieces.append(
            lax.dynamic_index_in_dim(source, global_block // row_count, axis=1, keepdims=False)
        )
    return jnp.concatenate(pieces, axis=1)


def local(child_front, top_front, block_map, pivots, noise, top_sample):
    row_count = lax.axis_size("row")
    col_count = lax.axis_size("col")
    group_count = lax.axis_size("group")
    my_row = lax.axis_index("row")
    my_col = lax.axis_index("col")
    my_group = lax.axis_index("group")
    block_rows = child_front.shape[3]
    panel_width = block_rows * col_count
    pivot_total = noise.shape[1]
    child_cols = child_front.shape[1]
    child_rows = child_front.shape[4]
    root_count = row_count // math.gcd(row_count, col_count)
    local_tile = child_front.reshape(child_cols * block_rows, child_rows * block_rows)
    col_index = global_index(child_cols, col_count, my_col, block_rows)
    row_index = global_index(child_rows, row_count, my_row, block_rows)
    live_count = pivots[0]
    dead_cols = (col_index < pivot_total) & (col_index >= live_count)
    dead_rows = (row_index < pivot_total) & (row_index >= live_count)
    keep_mask = jnp.logical_not(dead_cols)[:, None] & jnp.logical_not(dead_rows)[None, :]
    unit_matrix = (col_index[:, None] == row_index[None, :]).astype(jnp.float32)
    local_tile = jnp.where(keep_mask, local_tile, unit_matrix)
    identity = jnp.eye(panel_width, dtype=jnp.float32)
    inverses = []
    for panel_index in range(pivot_total // panel_width):
        panel_piece = local_tile[panel_index * block_rows : (panel_index + 1) * block_rows]
        panel_rows = lax.all_gather(panel_piece, "col", axis=0, tiled=True)
        first_block = panel_index * col_count // row_count
        last_block = ((panel_index + 1) * col_count - 1) // row_count + 1
        own_piece = panel_rows[:, first_block * block_rows : last_block * block_rows][:, None]
        gathered = gather_directly(own_piece, "row", 1)
        diagonal = diagonal_from_rows(
            gathered, panel_index, first_block, row_count, col_count, block_rows
        )
        factor = jnp.linalg.cholesky(diagonal)
        inverse = lax.linalg.triangular_solve(factor, identity, left_side=True, lower=True)
        lower_rows = jnp.dot(inverse, panel_rows, precision=HIGH)
        lower_rows = jnp.where(row_index[None, :] >= panel_index * panel_width, lower_rows, 0.0)
        received = []
        for source_step in range(root_count):
            root_index = (my_col + col_count * source_step) % row_count
            arrival = from_root(lower_rows, "row", root_index)
            received.append(arrival.reshape(panel_width, child_rows, block_rows))
        column_rows = pick_columns(received, child_cols, my_col, row_count, col_count)
        local_tile = local_tile - cross_product(column_rows, lower_rows)
        own_rows = lax.dynamic_slice_in_dim(lower_rows, my_col * block_rows, block_rows, 0)
        local_tile = local_tile.at[panel_index * block_rows : (panel_index + 1) * block_rows].set(
            own_rows
        )
        inverses.append(inverse)
    update_col = pivot_total // panel_width
    update_row = pivot_total // (block_rows * row_count)
    pivot_blocks = pivot_total // block_rows
    col_updates = child_cols - update_col
    row_updates = child_rows - update_row
    schur_part = local_tile[update_col * block_rows :, update_row * block_rows :]
    col_blocks = (
        jnp.arange(update_col, child_cols, dtype=jnp.int32) * col_count + my_col - pivot_blocks
    )
    row_blocks = (
        jnp.arange(update_row, child_rows, dtype=jnp.int32) * row_count + my_row - pivot_blocks
    )
    top_cols = top_front.shape[0]
    share = top_front.shape[3]
    top_rows = top_front.shape[4]
    col_target = jnp.take(block_map, col_blocks, axis=1) // col_count
    row_target = jnp.take(block_map, row_blocks, axis=1) // row_count
    col_hot = (
        col_target[:, :, None] == jnp.arange(top_cols, dtype=jnp.int32)[None, None, :]
    ).astype(jnp.float32)
    row_hot = (
        row_target[:, :, None] == jnp.arange(top_rows, dtype=jnp.int32)[None, None, :]
    ).astype(jnp.float32)
    top_tile = top_front.reshape(top_cols, share, top_rows, block_rows)
    shares = schur_part.reshape(col_updates, group_count, share, row_updates, block_rows)
    arrived = lax.all_to_all(shares, "group", split_axis=1, concat_axis=1, tiled=True)
    placed = jnp.einsum("gbl,agmbi->gamli", row_hot, arrived, precision=HIGH)
    top_tile = top_tile + jnp.einsum("gak,gamli->kmli", col_hot, placed, precision=HIGH)
    top_out = top_tile.reshape(top_front.shape)
    my_map = lax.dynamic_index_in_dim(block_map, my_group, 0, keepdims=False)
    coupled = jnp.take(
        top_sample.reshape(-1, block_rows), jnp.take(my_map, row_blocks), axis=0
    ).reshape(-1)
    pivot_rows = jnp.arange(update_row, dtype=jnp.int32) * row_count + my_row
    solved = jnp.zeros((pivot_total,), jnp.float32)
    for panel_index in reversed(range(pivot_total // panel_width)):
        known = jnp.take(solved.reshape(-1, block_rows), pivot_rows, axis=0).reshape(-1)
        weights = jnp.concatenate([known, coupled])
        weights = jnp.where(row_index >= (panel_index + 1) * panel_width, weights, 0.0)
        partial_sum = jnp.dot(
            local_tile[panel_index * block_rows : (panel_index + 1) * block_rows],
            weights,
            precision=HIGH,
        )
        summed = taken_together(partial_sum, "row")
        panel_sum = lax.all_gather(summed, "col", axis=0, tiled=True)
        right_side = (
            noise[0, panel_index * panel_width : (panel_index + 1) * panel_width] - panel_sum
        )
        update = jnp.dot(right_side, inverses[panel_index], precision=HIGH)
        solved = solved.at[panel_index * panel_width : (panel_index + 1) * panel_width].set(update)
    return (top_out, solved[None, :])


def solution(mesh):
    return jax.shard_map(
        local,
        mesh=mesh,
        in_specs=(
            P("group", None, "col", None, None, "row", None),
            P(None, "col", "group", None, None, "row", None),
            P(),
            P("group"),
            P("group", None),
            P(),
        ),
        out_specs=(P(None, "col", "group", None, None, "row", None), P("group", None)),
        check_vma=False,
    )
```

profile of v0, /device:TPU:8, one launch (start us, length us, event | category | flops | bytes accessed | tf_op | source)
XLA Modules:
  0.0 536.8 jit_solution(13807276972668406092)
XLA Ops:
  9.4 15.4 %all_gather.28 = f32[512,256]{1,0:T(8,128)S(1)} all-gather(f32[128,256]{1,0:T(8,128)S(1)} %slice.263), channel_id=1, replica_groups=mesh['group'=16,'row'=8,'col'=4] {'col'}, dimensions={0}, use_global_device_ids=true | all-gather | bytes 655360 | tf_op jit(solution)/shard_map/all_gather | solution.py:91
  24.9 1.6 broadcast_in_dim.98
  26.5 3.6 all-to-all-start
  30.3 26.9 %all-to-all-done = f32[8,512,1,128]{1,3,2,0:T(8,128)S(1)} async-done(((f32[8,512,1,128]{1,3,2,0:T(8,128)}), f32[8,512,1,128]{1,3,2,0:T(8,128)S(1)}, u32[]{:S(2)}, u32[]{:S(2)}) %all-to-all-start) | async-done | bytes 2097184 | tf_op jit(solution)/shard_map/all_to_all | solution.py:19
  58.3 2.6 copy.33
  60.9 1.4 fusion.17
  63.3 11.7 %cholesky.286 = f32[128,128]{1,0:T(8,128)S(1)} custom-call(f32[128,128]{1,0:T(8,128)S(1)} %cholesky.426), custom_call_target="Cholesky" | custom-call | tf_op jit(solution)/shard_map/jit(cholesky)/cholesky | solution.py:99
  75.1 9.8 %custom-call.27 = f32[1,128,128]{1,2,0:T(8,128)S(1)} custom-call(f32[1,128,128]{2,1,0:T(8,128)S(1)} %get-tuple-element.172), custom_call_target="InvertDiagBlocksLowerTriangular" | custom-call | tf_op jit(solution)/shard_map/jit(cholesky)/cholesky | solution.py:99
  87.5 11.7 %cholesky.305 = f32[128,128]{1,0:T(8,128)S(1)} custom-call(f32[128,128]{1,0:T(8,128)S(1)} %cholesky.430), custom_call_target="Cholesky" | custom-call | tf_op jit(solution)/shard_map/jit(cholesky)/cholesky | solution.py:99
  100.6 10.0 %custom-call.28 = f32[1,128,128]{1,2,0:T(8,128)S(1)} custom-call(f32[1,128,128]{2,1,0:T(8,128)S(1)} %get-tuple-element.169), custom_call_target="InvertDiagBlocksLowerTriangular" | custom-call | tf_op jit(solution)/shard_map/jit(cholesky)/cholesky | solution.py:99
  112.2 11.7 %cholesky.326 = f32[128,128]{1,0:T(8,128)S(1)} custom-call(f32[128,128]{1,0:T(8,128)S(1)} %cholesky.435), custom_call_target="Cholesky" | custom-call | tf_op jit(solution)/shard_map/jit(cholesky)/cholesky | solution.py:99
  124.6 9.8 %custom-call.29 = f32[1,128,128]{1,2,0:T(8,128)S(1)} custom-call(f32[1,128,128]{2,1,0:T(8,128)S(1)} %get-tuple-element.166), custom_call_target="InvertDiagBlocksLowerTriangular" | custom-call | tf_op jit(solution)/shard_map/jit(cholesky)/cholesky | solution.py:99
  135.8 12.1 %cholesky.343 = f32[128,128]{1,0:T(8,128)S(1)} custom-call(f32[128,128]{1,0:T(8,128)S(1)} %convolution_subtract_fusion.13), custom_call_target="Cholesky" | custom-call | tf_op jit(solution)/shard_map/jit(cholesky)/cholesky | solution.py:99
  151.2 8.2 %while.12 = (s32[]{:T(128)}, f32[512,512]{1,0:T(8,128)S(1)}, s32[4,2]{0,1:T(2,128)S(1)}, f32[4,128,128]{2,1,0:T(8,128)S(1)}, s32[]{:T(128)}) while((s32[]{:T(128)}, f32[512,512]{1,0:T(8,128)S(1)}, s32[4,2]{0,1:T(2,128)S(1)}, f32[4,128,128]{2,1,0:T(8,128)S(1)}, s32[]{:T(128)}) %tuple.106), condition=%wide.while_cond.4, body=%wide.while_body.4.sunk | while | flops 2 | bytes 131181 | solution.py:100
  151.9 1.4 bitcast_dynamic-update-slice_fusion.4
  159.4 39.3 %custom-call.30 = f32[4,128,128]{1,2,0:T(8,128)S(1)} custom-call(f32[4,128,128]{2,1,0:T(8,128)S(1)} %get-tuple-element.111), custom_call_target="InvertDiagBlocksLowerTriangular" | custom-call | tf_op jit(solution)/shard_map/triangular_solve/custom-call.3 | solution.py:100
  201.9 1.8 convolution_select_fusion.1
  203.8 41.0 %all-gather.7.cloned.1.call-done = f32[4096,256]{1,0:T(8,128)} async-done(((f32[512,256]{1,0:T(8,128)}), f32[4096,256]{1,0:T(8,128)}) %all-gather.7.cloned.1.call-update) | async-done | bytes 4194320 | tf_op jit(solution)/shard_map/all_gather | solution.py:27
  244.8 2.1 constant_dynamic-slice_fusion.16
  249.4 1.8 convolution_subtract_fusion.1
  252.1 13.4 %all_gather.31 = f32[512,256]{1,0:T(8,128)S(1)} all-gather(f32[128,256]{1,0:T(8,128)S(1)} %slice.277), channel_id=1, replica_groups=mesh['group'=16,'row'=8,'col'=4] {'col'}, dimensions={0}, use_global_device_ids=true | all-gather | bytes 655360 | tf_op jit(solution)/shard_map/all_gather | solution.py:91
  266.5 1.6 broadcast_in_dim.101
  268.2 3.6 all-to-all-start.1
  272.0 26.9 %all-to-all-done.1 = f32[8,512,1,128]{1,3,2,0:T(8,128)S(1)} async-done(((f32[8,512,1,128]{1,3,2,0:T(8,128)}), f32[8,512,1,128]{1,3,2,0:T(8,128)S(1)}, u32[]{:S(2)}, u32[]{:S(2)}) %all-to-all-start.1) | async-done | bytes 2097184 | tf_op jit(solution)/shard_map/all_to_all | solution.py:19
  299.9 2.6 copy.35
  302.5 1.4 fusion.16
  304.9 11.7 %cholesky.358 = f32[128,128]{1,0:T(8,128)S(1)} custom-call(f32[128,128]{1,0:T(8,128)S(1)} %cholesky.439), custom_call_target="Cholesky" | custom-call | tf_op jit(solution)/shard_map/jit(cholesky)/cholesky | solution.py:99
  316.8 9.8 %custom-call.31 = f32[1,128,128]{1,2,0:T(8,128)S(1)} custom-call(f32[1,128,128]{2,1,0:T(8,128)S(1)} %get-tuple-element.162), custom_call_target="InvertDiagBlocksLowerTriangular" | custom-call | tf_op jit(solution)/shard_map/jit(cholesky)/cholesky | solution.py:99
  329.1 11.7 %cholesky.377 = f32[128,128]{1,0:T(8,128)S(1)} custom-call(f32[128,128]{1,0:T(8,128)S(1)} %cholesky.443), custom_call_target="Cholesky" | custom-call | tf_op jit(solution)/shard_map/jit(cholesky)/cholesky | solution.py:99
  342.2 10.2 %custom-call.32 = f32[1,128,128]{1,2,0:T(8,128)S(1)} custom-call(f32[1,128,128]{2,1,0:T(8,128)S(1)} %get-tuple-element.159), custom_call_target="InvertDiagBlocksLowerTriangular" | custom-call | tf_op jit(solution)/shard_map/jit(cholesky)/cholesky | solution.py:99
  353.9 11.7 %cholesky.398 = f32[128,128]{1,0:T(8,128)S(1)} custom-call(f32[128,128]{1,0:T(8,128)S(1)} %cholesky.448), custom_call_target="Cholesky" | custom-call | tf_op jit(solution)/shard_map/jit(cholesky)/cholesky | solution.py:99
  366.4 9.8 %custom-call.33 = f32[1,128,128]{1,2,0:T(8,128)S(1)} custom-call(f32[1,128,128]{2,1,0:T(8,128)S(1)} %get-tuple-element.156), custom_call_target="InvertDiagBlocksLowerTriangular" | custom-call | tf_op jit(solution)/shard_map/jit(cholesky)/cholesky | solution.py:99
  377.6 11.7 %cholesky.415 = f32[128,128]{1,0:T(8,128)S(1)} custom-call(f32[128,128]{1,0:T(8,128)S(1)} %convolution_subtract_fusion.12), custom_call_target="Cholesky" | custom-call | tf_op jit(solution)/shard_map/jit(cholesky)/cholesky | solution.py:99
  392.8 8.1 %while.13 = (s32[]{:T(128)}, f32[512,512]{1,0:T(8,128)S(1)}, s32[4,2]{0,1:T(2,128)S(1)}, f32[4,128,128]{2,1,0:T(8,128)S(1)}, s32[]{:T(128)}) while((s32[]{:T(128)}, f32[512,512]{1,0:T(8,128)S(1)}, s32[4,2]{0,1:T(2,128)S(1)}, f32[4,128,128]{2,1,0:T(8,128)S(1)}, s32[]{:T(128)}) %tuple.116), condition=%wide.while_cond.4.clone, body=%wide.while_body.4.clone.sunk | while | flops 2 | bytes 131181 | solution.py:100
  400.9 39.3 %custom-call.34 = f32[4,128,128]{1,2,0:T(8,128)S(1)} custom-call(f32[4,128,128]{2,1,0:T(8,128)S(1)} %get-tuple-element.112), custom_call_target="InvertDiagBlocksLowerTriangular" | custom-call | tf_op jit(solution)/shard_map/triangular_solve/custom-call.3 | solution.py:100
  446.3 1.8 convolution_select_fusion
  451.9 3.3 all-to-all-start.3
  455.8 4.6 all-to-all-done.3
  460.4 7.2 %all-gather.2 = f32[4,1,128]{2,1,0:T(1,128)S(1)} all-gather(f32[1,1,128]{2,1,0:T(1,128)S(1)} %bitcast.249), channel_id=1, replica_groups=mesh['group'=16,'row'=8,'col'=4] {'col'}, dimensions={0}, use_global_device_ids=true | all-gather | bytes 2560 | tf_op jit(solution)/shard_map/all_gather | solution.py:160
  467.5 1.6 fusion.31
  469.2 17.9 %all-gather.9.cloned.1.call-done = f32[4096,256]{1,0:T(8,128)} async-done(((f32[512,256]{1,0:T(8,128)}), f32[4096,256]{1,0:T(8,128)}) %all-gather.9.cloned.1.call-update) | async-done | bytes 4194320 | tf_op jit(solution)/shard_map/all_gather | solution.py:27
  489.9 1.8 convolution_subtract_fusion
  492.6 3.3 all-to-all-start.4
  496.7 4.4 all-to-all-done.4
  501.1 12.3 %all-to-all-start.2 = ((f32[2,16,8,1,128]{4,2,0,3,1:T(8,128)}), f32[2,16,8,1,128]{4,2,0,3,1:T(8,128)S(1)}, u32[]{:S(2)}, u32[]{:S(2)}) async-start(f32[2,16,8,1,128]{4,2,0,3,1:T(8,128)} %copy.36), calls=%async_computation.2 | async-start | bytes 262144 | tf_op jit(solution)/shard_map/all_to_all | solution.py:140
  513.4 7.8 %all-gather.3 = f32[4,1,128]{2,1,0:T(1,128)S(1)} all-gather(f32[1,1,128]{2,1,0:T(1,128)S(1)} %bitcast.248), channel_id=1, replica_groups=mesh['group'=16,'row'=8,'col'=4] {'col'}, dimensions={0}, use_global_device_ids=true | all-gather | bytes 2560 | tf_op jit(solution)/shard_map/all_gather | solution.py:160
  521.3 1.6 convolution_dynamic-update-slice_fusion.4
  522.9 5.2 all-to-all-done.2
  (180 shorter events, 61.0 us)
Async XLA Ops:
  9.4 17.2 %copy-start.4 = (f32[512,256]{1,0:T(8,128)}, f32[512,256]{1,0:T(8,128)S(1)}, u32[]{:S(2)}) copy-start(f32[512,256]{1,0:T(8,128)S(1)} %bitcast_select_fusion) | copy-start | bytes 1572868
  24.8 1.8 copy-start.10
  26.5 30.7 %all-to-all-start = ((f32[8,512,1,128]{1,3,2,0:T(8,128)}), f32[8,512,1,128]{1,3,2,0:T(8,128)S(1)}, u32[]{:S(2)}, u32[]{:S(2)}) async-start(f32[8,512,1,128]{1,3,2,0:T(8,128)} %broadcast_in_dim.98), calls=%async_computation | async-start | bytes 4194304 | tf_op jit(solution)/shard_map/all_to_all | solution.py:19
  30.2 214.6 %all-gather.7.cloned.1.call-start = ((), (), s32[]{:S(2)}) async-start(), calls=%async_computation.5 | async-start | bytes 4718592 | tf_op jit(solution)/shard_map/all_gather | solution.py:27
  62.3 1.0 copy-start
  199.5 2.4 copy-start.11
  200.0 2.0 copy-start.8
  200.8 1.1 copy-start.15
  201.9 45.0 %copy-start.19 = (f32[128,512]{1,0:T(8,128)}, f32[128,512]{1,0:T(8,128)S(1)}, u32[]{:S(2)}) copy-start(f32[128,512]{1,0:T(8,128)S(1)} %fusion.68) | copy-start | bytes 786436
  246.9 2.5 copy-start.5
  246.9 2.6 copy-start.6
  251.3 0.8 copy-start.2
  265.6 0.8 copy-start.12
  268.2 30.7 %all-to-all-start.1 = ((f32[8,512,1,128]{1,3,2,0:T(8,128)}), f32[8,512,1,128]{1,3,2,0:T(8,128)S(1)}, u32[]{:S(2)}, u32[]{:S(2)}) async-start(f32[8,512,1,128]{1,3,2,0:T(8,128)} %broadcast_in_dim.101), calls=%async_computation.1 | async-start | bytes 4194304 | tf_op jit(solution)/shard_map/all_to_all | solution.py:19
  271.8 215.4 %all-gather.9.cloned.1.call-start = ((), (), s32[]{:S(2)}) async-start(), calls=%async_computation.6 | async-start | bytes 4718592 | tf_op jit(solution)/shard_map/all_gather | solution.py:27
  303.9 1.0 copy-start.1
  440.2 0.7 copy-start.18
  441.3 5.0 copy-start.13
  444.3 1.9 copy-start.16
  444.9 3.1 copy-start.14
  445.0 5.2 copy-start.20
  451.9 8.5 %all-to-all-start.3 = ((f32[8,1,128]{2,1,0:T(1,128)}), f32[8,1,128]{2,1,0:T(1,128)S(1)}, u32[]{:S(2)}, u32[]{:S(2)}) async-start(f32[8,1,128]{2,1,0:T(1,128)} %broadcast_in_dim.108), calls=%async_computation.3 | async-start | bytes 8192 | tf_op jit(solution)/shard_map/all_to_all | solution.py:19
  488.4 1.5 copy-start.3
  488.4 1.5 copy-start.7
  489.4 31.8 %copy-start.9 = (f32[128,512]{1,0:T(8,128)S(1)}, f32[128,512]{1,0:T(8,128)}, u32[]{:S(2)}) copy-start(f32[128,512]{1,0:T(8,128)} %copy-done.8) | copy-start | bytes 786436
  491.8 36.4 %copy-start.17 = (f32[12,1,1,8,6,1,128]{6,5,4,3,2,1,0:T(1,128)S(1)}, f32[12,1,1,8,6,1,128]{6,5,4,3,2,1,0:T(1,128)}, u32[]{:S(2)}) copy-start(f32[12,1,1,8,6,1,128]{6,5,4,3,2,1,0:T(1,128)} %param.20) | copy-start | bytes 884740
  492.6 8.5 %all-to-all-start.4 = ((f32[8,1,128]{2,1,0:T(1,128)}), f32[8,1,128]{2,1,0:T(1,128)S(1)}, u32[]{:S(2)}, u32[]{:S(2)}) async-start(f32[8,1,128]{2,1,0:T(1,128)} %broadcast_in_dim.110), calls=%async_computation.4 | async-start | bytes 8192 | tf_op jit(solution)/shard_map/all_to_all | solution.py:19
  501.1 27.1 %all-to-all-start.2 = ((f32[2,16,8,1,128]{4,2,0,3,1:T(8,128)}), f32[2,16,8,1,128]{4,2,0,3,1:T(8,128)S(1)}, u32[]{:S(2)}, u32[]{:S(2)}) async-start(f32[2,16,8,1,128]{4,2,0,3,1:T(8,128)} %copy.36), calls=%async_computation.2 | async-start | bytes 262144 | tf_op jit(solution)/shard_map/all_to_all | solution.py:140
  522.9 6.8 %copy-start.21 = (f32[1,1024]{1,0:T(1,128)}, f32[1,1024]{1,0:T(1,128)S(1)}, u32[]{:S(2)}) copy-start(f32[1,1024]{1,0:T(1,128)S(1)} %convolution_dynamic-update-slice_fusion.4) | copy-start | bytes 12292
Sparse Core Ops, SparseCore 0:
  203.9 40.8 all-gather.6
  448.2 38.8 all-gather.8
where the time goes:
time: 547 us; the launch traced here: 537 us
  other arithmetic  243 us (44%)
  waiting for transfers between devices  127 us (23%)
  blocking collectives  43.8 us (8%)
  local copies, waits for them, and re-layouts  42.6 us (8%)
  matrix products  31.9 us (6%)
  starting transfers between devices  26.4 us (5%)
  between operations  21.5 us (4%)
    another operation x30, other arithmetic, local(): factor = jnp.linalg.cholesky(diagonal)  159 us
    another operation x5, other arithmetic, local(): lax.linalg.triangular_solve(factor, identity, left_side=True, lower=True)  78.9 us
    all_to_all x4, waiting for transfers between devices, from_everyone(): return lax.all_to_all(copies, axis, split_axis=0, concat_axis=0, tiled=True)  62.7 us
    all_gather x2, waiting for transfers between devices, from_root(): lax.all_gather(value, axis)  58.9 us
    all_gather x2, blocking collectives, local(): panel_rows = lax.all_gather(panel_piece, 'col', axis=0, tiled=True)  28.8 us
    another operation x27, local copies, waits for them, and re-layouts, local(): lax.linalg.triangular_solve(factor, identity, left_side=True, lower=True)  16.1 us
    all_gather x2, blocking collectives, local(): panel_sum = lax.all_gather(summed, 'col', axis=0, tiled=True)  15 us
    all_to_all x4, starting transfers between devices, from_everyone(): return lax.all_to_all(copies, axis, split_axis=0, concat_axis=0, tiled=True)  13.8 us
  transfers between devices with their start and end apart: 7, of which 7 were waited for; matrix products, arithmetic and copies ran while one was open for 1% of the time, Pallas kernels for 0%

commit v1 on v0

v1 whole, which is shorter than its diff:
```python
import functools

import jax
import jax.numpy as jnp
from jax import lax
from jax.experimental import pallas as pl
from jax.experimental.pallas import tpu as pltpu
from jax.sharding import PartitionSpec as P

HIGH = lax.Precision.HIGHEST
F32 = jnp.float32
BF16 = jnp.bfloat16
B = 128
G = 8
PAIRS = [(i, i ^ 1) for i in range(8)]
PARITY = [[0, 2, 4, 6], [1, 3, 5, 7]]


def halves(x):
    high = x.astype(BF16)
    return high, (x - high.astype(F32)).astype(BF16)


def dot3(left, right, dims):
    lh, ll = halves(left)
    rh, rl = halves(right)

    def part(p, q):
        return lax.dot_general(p, q, (dims, ((), ())), preferred_element_type=F32)

    return part(lh, rh) + (part(lh, rl) + part(ll, rh))


def factor_block(vs):
    n = len(vs)
    sub = lax.broadcasted_iota(jnp.int32, (G, B), 0)
    lane = lax.broadcasted_iota(jnp.int32, (G, B), 1)
    vs = list(vs)
    out = []
    for g in range(n):
        base = g * G
        ingroup = (lane >= base) & (lane < base + G)
        cols = {}
        for v in range(g, n):
            for c in range(G):
                cols[v, c] = jnp.broadcast_to(vs[v][:, base + c : base + c + 1], (G, B))
        vs[g] = jnp.where(ingroup, jnp.where(lane - base == sub, 1.0, 0.0), vs[g])
        for v in range(g + 1, n):
            vs[v] = jnp.where(ingroup, 0.0, vs[v])
        dvec = jnp.ones((G, B), F32)
        for j in range(G):
            d = jnp.broadcast_to(cols[g, j][j : j + 1, :], (G, B))
            r = 1.0 / d
            dvec = jnp.where(sub == j, d, dvec)
            us = [
                jnp.broadcast_to(cols[g, c][j : j + 1, :], (G, B)) for c in range(j + 1, G)
            ]
            row = jnp.broadcast_to(vs[g][j : j + 1, :], (G, B))
            for v in range(g, n):
                f = cols[v, j] * r
                if v == g:
                    f = jnp.where(sub > j, f, 0.0)
                for i, c in enumerate(range(j + 1, G)):
                    cols[v, c] = cols[v, c] - f * us[i]
                vs[v] = vs[v] - f * row
        out.append(jnp.where(lane - base <= sub, vs[g] * lax.rsqrt(dvec), 0.0))
    return out


def child_kernel(
    par_ref, o0, o1, o2, q0, q1, q2, e_ref, co_ref, cq_ref, m_ref, n_ref,
    s_ref, x_ref, a_ref, lin_ref,
):
    nb = 8
    n = 12 * B
    even = par_ref[0] == 0
    owns, others = (o0, o1, o2), (q0, q1, q2)

    def rows_of(x, c, lo, hi):
        mine, theirs = [], []
        for p in range(3):
            a, b = max(lo, 88 * p), min(hi, 88 * p + 88)
            if a < b:
                mine.append(owns[p][x, c, a - 88 * p : b - 88 * p, :])
                theirs.append(others[p][x, c, a - 88 * p : b - 88 * p, :])
        mine = jnp.concatenate(mine, 0) if len(mine) > 1 else mine[0]
        theirs = jnp.concatenate(theirs, 0) if len(theirs) > 1 else theirs[0]
        return jnp.where(even, mine, theirs), jnp.where(even, theirs, mine)

    for c in range(4):
        sums = None
        for x in range(4):
            for lc in range(2):
                r0 = (4 * lc + c) * B
                b0, b1 = rows_of(x, c, lc * B, lc * B + B)
                a_ref[r0 : r0 + B, 2 * x * B : 2 * x * B + B] = b0
                a_ref[r0 : r0 + B, 2 * x * B + B : 2 * x * B + 2 * B] = b1
            t0, t1 = rows_of(x, c, 256, 264)
            sums = t0 + t1 if sums is None else sums + t0 + t1
        for lc in range(2):
            r0 = (4 * lc + c) * B
            a_ref[r0 : r0 + B, 11 * B :] = jnp.broadcast_to(sums[lc : lc + 1, :], (B, B)).T
            a_ref[r0 : r0 + B, 8 * B : 9 * B] = e_ref[c, lc * B : lc * B + B, :]
    for x in range(4):
        for lc in range(2):
            mine = co_ref[x, lc * B : lc * B + B, :]
            theirs = cq_ref[x, lc * B : lc * B + B, :]
            cs = slice((9 + lc) * B, (10 + lc) * B)
            a_ref[2 * x * B : 2 * x * B + B, cs] = jnp.where(even, mine, theirs).T
            a_ref[2 * x * B + B : 2 * x * B + 2 * B, cs] = jnp.where(even, theirs, mine).T

    def body(k, carry):
        off = pl.multiple_of(k * B, B)
        rows = factor_block(
            [a_ref[pl.ds(off + G * i, G), pl.ds(off, B)] for i in range(B // G)]
        )
        for i in range(B // G):
            lin_ref[pl.ds(off + G * i, G), :] = rows[i]
        for kk in range(nb):

            @pl.when(k == kk)
            def _():
                s, m = (kk + 1) * B, nb * B
                lin = lin_ref[kk * B : s, :]
                w = dot3(lin, a_ref[kk * B : s, s:], ((1,), (0,)))
                a_ref[kk * B : s, s:] = w
                if s < m:
                    low = dot3(a_ref[s:m, kk * B : s], lin, ((1,), (1,)))
                    a_ref[s:m, s:] = a_ref[s:m, s:] - dot3(low, w, ((1,), (0,)))

        return carry

    lax.fori_loop(0, nb, body, 0)

    prod = dot3(a_ref[:, 9 * B : 11 * B], a_ref[:, 8 * B : 9 * B], ((0,), (0,)))
    for b in range(2):
        for p in range(16):
            lo = b * B + G * p
            s_ref[p, b, :, :] = m_ref[lo : lo + G, :] - prod[lo : lo + G, :]

    xs = [None] * nb
    for k in reversed(range(nb)):
        ks = slice(k * B, k * B + B)
        z = jnp.broadcast_to(n_ref[:, ks], (B, B)).T - a_ref[ks, 11 * B :]
        if k + 1 < nb:
            acc = None
            for j in range(k + 1, nb):
                term = a_ref[ks, j * B : j * B + B] * xs[j]
                acc = term if acc is None else acc + term
            z = z - jnp.sum(acc, axis=1, keepdims=True)
        xs[k] = jnp.sum(lin_ref[ks, :] * z, axis=0, keepdims=True)
        x_ref[:, ks] = xs[k]


def local(child_front, top_front, block_map, pivots, noise, top_sample):
    my_row = lax.axis_index("row")
    my_col = lax.axis_index("col")
    my_group = lax.axis_index("group")
    pivot_total = noise.shape[1]
    tile = child_front.reshape(4, B, 2, B)
    live = pivots[0]
    lane = jnp.arange(B, dtype=jnp.int32)
    col_index = ((jnp.arange(4, dtype=jnp.int32) * 4 + my_col) * B)[:, None] + lane[None, :]
    row_index = ((jnp.arange(2, dtype=jnp.int32) * 8 + my_row) * B)[:, None] + lane[None, :]
    dead_c = (col_index < pivot_total) & (col_index >= live)
    dead_r = (row_index < pivot_total) & (row_index >= live)
    dead = dead_c[:, :, None, None] | dead_r[None, None, :, :]
    unit = (col_index[:, :, None, None] == row_index[None, None, :, :]).astype(F32)
    tile = jnp.where(dead, unit, tile)
    my_map = lax.dynamic_index_in_dim(block_map, my_group, 0, keepdims=False)
    known = lax.dynamic_index_in_dim(
        top_sample.reshape(-1, B), lax.dynamic_index_in_dim(my_map, my_row, 0, keepdims=False), 0
    )
    cross = tile[0:2, :, 1, :]
    partial_sum = jnp.sum(cross * known[None], axis=-1)
    first = jnp.concatenate(
        [tile[0:2, :, 0, :].reshape(2 * B, B), partial_sum, jnp.zeros((6, B), F32)], axis=0
    )
    wide = lax.all_gather(first, "col")
    cross_all = lax.all_gather(cross.reshape(2 * B, B), "col")
    own, other = [], []
    for p in range(3):
        got = lax.all_gather(wide[:, 88 * p : 88 * p + 88], "row", axis_index_groups=PARITY)
        own.append(got)
        other.append(lax.ppermute(got, "row", PAIRS))
    cols_own = lax.all_gather(
        tile[2:4, :, 0, :].reshape(2 * B, B), "row", axis_index_groups=PARITY
    )
    cols_other = lax.ppermute(cols_own, "row", PAIRS)
    vmem = pl.BlockSpec(memory_space=pltpu.VMEM)
    shares, solved = pl.pallas_call(
        child_kernel,
        out_shape=[
            jax.ShapeDtypeStruct((16, 2, G, B), F32),
            jax.ShapeDtypeStruct((1, pivot_total), F32),
        ],
        in_specs=[pl.BlockSpec(memory_space=pltpu.SMEM)] + [vmem] * 11,
        out_specs=[vmem, vmem],
        scratch_shapes=[pltpu.VMEM((8 * B, 12 * B), F32), pltpu.VMEM((8 * B, B), F32)],
        compiler_params=pltpu.CompilerParams(vmem_limit_bytes=48 * 2**20),
        name="child_front",
    )(
        (my_row % 2).astype(jnp.int32).reshape(1),
        *own,
        *other,
        cross_all,
        cols_own,
        cols_other,
        tile[2:4, :, 1, :].reshape(2 * B, B),
        noise,
    )
    arrived = lax.all_to_all(shares, "group", split_axis=0, concat_axis=0, tiled=True)

    col_blocks = jnp.arange(2, dtype=jnp.int32) * 4 + my_col
    col_target = jnp.take(block_map, col_blocks, axis=1) // 4
    row_target = lax.dynamic_index_in_dim(block_map, my_row, 1, keepdims=False) // 8
    top_cols = top_front.shape[0]
    top_rows = top_front.shape[4]
    col_hot = (
        col_target[:, :, None] == jnp.arange(top_cols, dtype=jnp.int32)[None, None, :]
    ).astype(F32)
    row_hot = (
        row_target[:, None] == jnp.arange(top_rows, dtype=jnp.int32)[None, :]
    ).astype(F32)
    top_tile = top_front.reshape(top_cols, G, top_rows, B)
    placed = row_hot[:, None, None, :, None] * arrived[:, :, :, None, :]
    top_tile = top_tile + jnp.einsum("gak,gamli->kmli", col_hot, placed, precision=HIGH)
    return (top_tile.reshape(top_front.shape), solved)


def solution(mesh):
    return jax.shard_map(
        local,
        mesh=mesh,
        in_specs=(
            P("group", None, "col", None, None, "row", None),
            P(None, "col", "group", None, None, "row", None),
            P(),
            P("group"),
            P("group", None),
            P(),
        ),
        out_specs=(P(None, "col", "group", None, None, "row", None), P("group", None)),
        check_vma=False,
    )
```

time: 547 us -> 180 us (0.33)
  the two profiles are of different devices: /device:TPU:8 before, /device:TPU:2 now
where the time goes in v1:
time: 180 us
  blocking collectives  84.6 us (47%)
  Pallas kernels  47.8 us (27%)
  starting transfers between devices  21.4 us (12%)
  waiting for transfers between devices  13.2 us (7%)
  local copies, waits for them, and re-layouts  5.44 us (3%)
  other arithmetic  3.52 us (2%)
  between operations  3.25 us (2%)
    pallas_call x1, Pallas kernels, local(): pl.pallas_call(child_kernel, out_shape=[jax.ShapeDtypeStruct((16, 2, G, B...  47.8 us
    all_gather x3, blocking collectives, local(): lax.all_gather(wide[:, 88 * p:88 * p + 88], 'row', axis_index_groups=PARITY)  43.9 us
    all_gather x1, blocking collectives, local(): cross_all = lax.all_gather(cross.reshape(2 * B, B), 'col')  13.8 us
    all_to_all x1, starting transfers between devices, local(): lax.all_to_all(shares, 'group', split_axis=0, concat_axis=0, tiled=True)  13.8 us
    all_gather x1, blocking collectives, local(): lax.all_gather(tile[2:4, :, 0, :].reshape(2 * B, B), 'row', axis_index_gr...  13.6 us
    all_gather x1, blocking collectives, local(): wide = lax.all_gather(first, 'col')  13.3 us
    all_to_all x1, waiting for transfers between devices, local(): lax.all_to_all(shares, 'group', split_axis=0, concat_axis=0, tiled=True)  13.2 us
    ppermute x3, starting transfers between devices, local(): other.append(lax.ppermute(got, 'row', PAIRS))  5.73 us
  transfers between devices with their start and end apart: 5, of which 1 were waited for; matrix products, arithmetic and copies ran while one was open for 0% of the time, Pallas kernels for 0%

profile of v1, /device:TPU:2, one launch (start us, length us, event | category | flops | bytes accessed | tf_op | source)
XLA Modules:
  0.0 179.8 jit_solution(775911080438262380)
XLA Ops:
  0.6 0.0 copy-start
  0.7 0.0 copy-start.5
  0.7 0.7 copy-done.5
  1.4 0.6 dynamic_slice.15
  3.7 0.1 iota_add_fusion.1
  3.8 0.1 compare_and_fusion
  3.9 0.1 iota_add_fusion
  4.0 0.1 compare_and_fusion.1
  4.0 2.9 %or_select_fusion = f32[4,128,2,128]{3,2,1,0:T(2,128)S(1)} fusion(f32[4,128,2,128]{3,2,1,0:T(2,128)} %bitcast.57, pred[2,128]{1,0:T(4,128)(4,1)S(1)} %compare_and_fusion, pred[4,128]{1,0:T(4,128)(4,1)S(1)} %compare_and_fusion.1, s32[2,128]{1,0:T(2,128)S(1)} %iota_add_fusion.1, s32[4,128]{1,0:T(4,128)S(1)} %iota_add_fusion), kind=kLoop, calls=%fused_computation.5 | loop fusion | flops 524288 | bytes 1052416 | tf_op jit(solution)/shard_map/jit(_where)/select_n | solution.py:169
  6.9 1.1 fusion.12
  8.0 0.0 copy-start.4
  8.6 0.0 copy-done
  8.6 0.1 multiply_reduce_fusion
  8.8 0.1 pad.2.clone
  8.8 0.1 maximum_maximum_fusion
  8.9 0.0 copy-done.4
  9.0 13.3 %all-gather = f32[1056,128]{1,0:T(8,128)S(1)} all-gather(f32[264,128]{1,0:T(8,128)S(1)} %maximum_maximum_fusion), channel_id=2, replica_groups=mesh['group'=16,'row'=8,'col'=4] {'col'}, dimensions={0}, use_global_device_ids=true | all-gather | bytes 675840 | tf_op jit(solution)/shard_map/all_gather | solution.py:179
  22.3 16.0 %all-gather.1 = f32[16,88,128]{2,1,0:T(8,128)S(1)} all-gather(f32[4,88,128]{2,1,0:T(8,128)S(1)} %get-tuple-element.12), channel_id=3, replica_groups={{0,8,16,24},{4,12,20,28},{1,9,17,25},{5,13,21,29},{2,10,18,26},{6,14,22..., dimensions={0}, use_global_device_ids=true | all-gather | bytes 901120 | tf_op jit(solution)/shard_map/all_gather | solution.py:183
  38.3 1.9 %collective-permute-start = (f32[4,4,88,128]{3,2,1,0:T(8,128)S(1)}, f32[4,4,88,128]{3,2,1,0:T(8,128)S(1)}, u32[]{:S(2)}, u32[]{:S(2)}) collective-permute-start(f32[4,4,88,128]{3,2,1,0:T(8,128)S(1)} %bitcast.47), channel_id=1, source_target_pairs={{0,4},{4,0},{8,12},{12,8},{16,20},{20,16},{24,28},{28,24},{1,5},{5... | collective-permute-start | bytes 2162696 | tf_op jit(solution)/shard_map/ppermute | solution.py:185
  40.2 13.7 %all-gather.2 = f32[16,88,128]{2,1,0:T(8,128)S(1)} all-gather(f32[4,88,128]{2,1,0:T(8,128)S(1)} %get-tuple-element.11), channel_id=4, replica_groups={{0,8,16,24},{4,12,20,28},{1,9,17,25},{5,13,21,29},{2,10,18,26},{6,14,22..., dimensions={0}, use_global_device_ids=true | all-gather | bytes 901120 | tf_op jit(solution)/shard_map/all_gather | solution.py:183
  53.9 1.9 %collective-permute-start.1 = (f32[4,4,88,128]{3,2,1,0:T(8,128)S(1)}, f32[4,4,88,128]{3,2,1,0:T(8,128)}, u32[]{:S(2)}, u32[]{:S(2)}) collective-permute-start(f32[4,4,88,128]{3,2,1,0:T(8,128)S(1)} %bitcast.49), channel_id=1, source_target_pairs={{0,4},{4,0},{8,12},{12,8},{16,20},{20,16},{24,28},{28,24},{1,5},{5... | collective-permute-start | bytes 2162696 | tf_op jit(solution)/shard_map/ppermute | solution.py:185
  55.8 0.0 copy-start.7
  55.8 14.2 %all-gather.3 = f32[16,88,128]{2,1,0:T(8,128)S(1)} all-gather(f32[4,88,128]{2,1,0:T(8,128)S(1)} %get-tuple-element.10), channel_id=5, replica_groups={{0,8,16,24},{4,12,20,28},{1,9,17,25},{5,13,21,29},{2,10,18,26},{6,14,22..., dimensions={0}, use_global_device_ids=true | all-gather | bytes 901120 | tf_op jit(solution)/shard_map/all_gather | solution.py:183
  70.0 1.9 %collective-permute-start.2 = (f32[4,4,88,128]{3,2,1,0:T(8,128)S(1)}, f32[4,4,88,128]{3,2,1,0:T(8,128)}, u32[]{:S(2)}, u32[]{:S(2)}) collective-permute-start(f32[4,4,88,128]{3,2,1,0:T(8,128)S(1)} %bitcast.51), channel_id=1, source_target_pairs={{0,4},{4,0},{8,12},{12,8},{16,20},{20,16},{24,28},{28,24},{1,5},{5... | collective-permute-start | bytes 2162696 | tf_op jit(solution)/shard_map/ppermute | solution.py:185
  72.0 0.0 copy-done.7
  72.0 13.6 %all_gather.39.co_ref = f32[4,256,128]{2,1,0:T(8,128)S(1)} all-gather(f32[1,256,128]{2,1,0:T(8,128)S(1)} %bitcast.58), channel_id=1, replica_groups={{0,8,16,24},{4,12,20,28},{1,9,17,25},{5,13,21,29},{2,10,18,26},{6,14,22..., dimensions={0}, use_global_device_ids=true | all-gather | bytes 655360 | tf_op jit(solution)/shard_map/all_gather | solution.py:186
  85.6 1.9 %collective-permute-start.3 = (f32[4,256,128]{2,1,0:T(8,128)S(1)}, f32[4,256,128]{2,1,0:T(8,128)}, u32[]{:S(2)}, u32[]{:S(2)}) collective-permute-start(f32[4,256,128]{2,1,0:T(8,128)S(1)} %all_gather.39.co_ref), channel_id=1, source_target_pairs={{0,4},{4,0},{8,12},{12,8},{16,20},{20,16},{24,28},{28,24},{1,5},{5... | collective-permute-start | bytes 1572872 | tf_op jit(solution)/shard_map/ppermute | solution.py:189
  87.5 0.0 copy-start.1
  87.5 13.8 %all_gather.38.e_ref = f32[4,256,128]{2,1,0:T(8,128)S(1)} all-gather(f32[1,256,128]{2,1,0:T(8,128)} %bitcast.56), channel_id=1, replica_groups=mesh['group'=16,'row'=8,'col'=4] {'col'}, dimensions={0}, use_global_device_ids=true | all-gather | bytes 655360 | tf_op jit(solution)/shard_map/all_gather | solution.py:180
  101.4 0.0 copy-start.3
  101.4 0.0 collective-permute-done.3.cq_ref
  101.4 0.0 collective-permute-done.q0
  101.4 0.0 collective-permute-done.1.q1
  101.4 0.0 collective-permute-done.2.q2
  101.4 0.0 copy-done.1
  101.4 0.6 copy-done.3
  102.1 47.8 %child_front.1 = (f32[16,2,8,128]{3,2,1,0:T(8,128)S(1)}, f32[1,1024]{1,0:T(1,128)}) custom-call(s32[1]{0:T(128)} %bitcast.6.par_ref, f32[4,4,88,128]{3,2,1,0:T(8,128)S(1)} %bitcast.48, f32[4,4,88,128]{3,2,1,0:T(8,128)S(1)} %bitcast.50, f32[4,4,88,128]{3,2,1,0:T(8,128)S(1)} %bitcast.52, f32[4,4,88,128]{3,2,1,0:T(8,128)S(1)} %collective-permute-done.q0, ...), custom_call_target="tpu_custom_call" | custom-call | tf_op jit(solution)/shard_map/child_front/pallas_call | solution.py:191
  149.9 0.0 copy-start.2
  149.9 0.7 copy-done.2
  150.5 0.0 copy-start.6
  150.5 13.8 %all-to-all-start = ((f32[16,2,8,128]{3,2,1,0:T(8,128)}), f32[16,2,8,128]{3,2,1,0:T(8,128)S(1)}, u32[]{:S(2)}, u32[]{:S(2)}) async-start(f32[16,2,8,128]{3,2,1,0:T(8,128)} %copy-done.2), calls=%async_computation | async-start | bytes 262144 | tf_op jit(solution)/shard_map/all_to_all | solution.py:212
  164.3 0.6 gather_fusion
  164.9 0.1 and_select_fusion.1
  165.0 13.2 %all-to-all-done = f32[16,2,8,128]{3,2,1,0:T(8,128)S(1)} async-done(((f32[16,2,8,128]{3,2,1,0:T(8,128)}), f32[16,2,8,128]{3,2,1,0:T(8,128)S(1)}, u32[]{:S(2)}, u32[]{:S(2)}) %all-to-all-start) | async-done | bytes 131104 | tf_op jit(solution)/shard_map/all_to_all | solution.py:212
  178.2 0.0 copy-done.6
  178.2 0.5 fusion.1
  178.8 1.0 copy.13
  (11 shorter events, 0.1 us)
Async XLA Ops:
  0.6 8.0 %copy-start = (f32[6144]{0:T(1024)S(1)}, f32[6144]{0:T(1024)}, u32[]{:S(2)}) copy-start(f32[6144]{0:T(1024)} %param.11) | copy-start | bytes 73732
  0.7 0.7 copy-start.5
  8.0 0.9 copy-start.4
  38.3 63.1 %collective-permute-start = (f32[4,4,88,128]{3,2,1,0:T(8,128)S(1)}, f32[4,4,88,128]{3,2,1,0:T(8,128)S(1)}, u32[]{:S(2)}, u32[]{:S(2)}) collective-permute-start(f32[4,4,88,128]{3,2,1,0:T(8,128)S(1)} %bitcast.47), channel_id=1, source_target_pairs={{0,4},{4,0},{8,12},{12,8},{16,20},{20,16},{24,28},{28,24},{1,5},{5... | collective-permute-start | bytes 2162696 | tf_op jit(solution)/shard_map/ppermute | solution.py:185
  53.9 47.5 %collective-permute-start.1 = (f32[4,4,88,128]{3,2,1,0:T(8,128)S(1)}, f32[4,4,88,128]{3,2,1,0:T(8,128)}, u32[]{:S(2)}, u32[]{:S(2)}) collective-permute-start(f32[4,4,88,128]{3,2,1,0:T(8,128)S(1)} %bitcast.49), channel_id=1, source_target_pairs={{0,4},{4,0},{8,12},{12,8},{16,20},{20,16},{24,28},{28,24},{1,5},{5... | collective-permute-start | bytes 2162696 | tf_op jit(solution)/shard_map/ppermute | solution.py:185
  55.8 16.1 %copy-start.7 = (f32[2,128,1,128]{3,2,1,0:T(1,128)S(1)}, f32[2,128,1,128]{3,2,1,0:T(1,128)}, u32[]{:S(2)}) copy-start(f32[2,128,1,128]{3,2,1,0:T(1,128)} %get-tuple-element.14) | copy-start | bytes 393220
  70.0 31.4 %collective-permute-start.2 = (f32[4,4,88,128]{3,2,1,0:T(8,128)S(1)}, f32[4,4,88,128]{3,2,1,0:T(8,128)}, u32[]{:S(2)}, u32[]{:S(2)}) collective-permute-start(f32[4,4,88,128]{3,2,1,0:T(8,128)S(1)} %bitcast.51), channel_id=1, source_target_pairs={{0,4},{4,0},{8,12},{12,8},{16,20},{20,16},{24,28},{28,24},{1,5},{5... | collective-permute-start | bytes 2162696 | tf_op jit(solution)/shard_map/ppermute | solution.py:185
  85.6 15.8 %collective-permute-start.3 = (f32[4,256,128]{2,1,0:T(8,128)S(1)}, f32[4,256,128]{2,1,0:T(8,128)}, u32[]{:S(2)}, u32[]{:S(2)}) collective-permute-start(f32[4,256,128]{2,1,0:T(8,128)S(1)} %all_gather.39.co_ref), channel_id=1, source_target_pairs={{0,4},{4,0},{8,12},{12,8},{16,20},{20,16},{24,28},{28,24},{1,5},{5... | collective-permute-start | bytes 1572872 | tf_op jit(solution)/shard_map/ppermute | solution.py:189
  87.5 13.9 %copy-start.1 = (f32[2,128,1,128]{3,2,1,0:T(1,128)S(1)}, f32[2,128,1,128]{3,2,1,0:T(1,128)}, u32[]{:S(2)}) copy-start(f32[2,128,1,128]{3,2,1,0:T(1,128)} %get-tuple-element.13) | copy-start | bytes 393220
  101.4 0.7 copy-start.3
  149.9 0.7 copy-start.2
  150.5 27.7 %copy-start.6 = (f32[12,1,1,8,6,1,128]{6,5,4,3,2,1,0:T(1,128)S(1)}, f32[12,1,1,8,6,1,128]{6,5,4,3,2,1,0:T(1,128)}, u32[]{:S(2)}) copy-start(f32[12,1,1,8,6,1,128]{6,5,4,3,2,1,0:T(1,128)} %param.7) | copy-start | bytes 884740
  150.5 27.6 %all-to-all-start = ((f32[16,2,8,128]{3,2,1,0:T(8,128)}), f32[16,2,8,128]{3,2,1,0:T(8,128)S(1)}, u32[]{:S(2)}, u32[]{:S(2)}) async-start(f32[16,2,8,128]{3,2,1,0:T(8,128)} %copy-done.2), calls=%async_computation | async-start | bytes 262144 | tf_op jit(solution)/shard_map/all_to_all | solution.py:212

commit v2 on v1

v2 whole, which is shorter than its diff:
```python
import functools

import jax
import jax.numpy as jnp
from jax import lax
from jax.experimental import pallas as pl
from jax.experimental.pallas import tpu as pltpu
from jax.sharding import PartitionSpec as P

HIGH = lax.Precision.HIGHEST
F32 = jnp.float32
BF16 = jnp.bfloat16
B = 128
G = 8
HEAD = B + 8
PAIRS = [(i, i ^ 1) for i in range(8)]
PARITY = [[0, 2, 4, 6], [1, 3, 5, 7]]


def halves(x):
    high = x.astype(BF16)
    return high, (x - high.astype(F32)).astype(BF16)


def dot3(left, right, dims):
    lh, ll = halves(left)
    rh, rl = halves(right)

    def part(p, q):
        return lax.dot_general(p, q, (dims, ((), ())), preferred_element_type=F32)

    return part(lh, rh) + (part(lh, rl) + part(ll, rh))


def factor_block(vs):
    n = len(vs)
    sub = lax.broadcasted_iota(jnp.int32, (G, B), 0)
    lane = lax.broadcasted_iota(jnp.int32, (G, B), 1)
    vs = list(vs)
    out = []
    for g in range(n):
        base = g * G
        ingroup = (lane >= base) & (lane < base + G)
        cols = {}
        for v in range(g, n):
            for c in range(G):
                cols[v, c] = jnp.broadcast_to(vs[v][:, base + c : base + c + 1], (G, B))
        vs[g] = jnp.where(ingroup, jnp.where(lane - base == sub, 1.0, 0.0), vs[g])
        for v in range(g + 1, n):
            vs[v] = jnp.where(ingroup, 0.0, vs[v])
        dvec = jnp.ones((G, B), F32)
        for j in range(G):
            d = jnp.broadcast_to(cols[g, j][j : j + 1, :], (G, B))
            r = 1.0 / d
            dvec = jnp.where(sub == j, d, dvec)
            us = [
                jnp.broadcast_to(cols[g, c][j : j + 1, :], (G, B)) for c in range(j + 1, G)
            ]
            row = jnp.broadcast_to(vs[g][j : j + 1, :], (G, B))
            for v in range(g, n):
                f = cols[v, j] * r
                if v == g:
                    f = jnp.where(sub > j, f, 0.0)
                for i, c in enumerate(range(j + 1, G)):
                    cols[v, c] = cols[v, c] - f * us[i]
                vs[v] = vs[v] - f * row
        out.append(jnp.where(lane - base <= sub, vs[g] * lax.rsqrt(dvec), 0.0))
    return out


def front_kernel(f_ref, map_ref, piv_ref, y_ref, first_ref, cols_ref):
    my_row = lax.axis_index("row")
    my_col = lax.axis_index("col")
    my_group = lax.axis_index("group")
    live = piv_ref[0]
    shape = (B, B)
    i_id = lax.broadcasted_iota(jnp.int32, shape, 0)
    t_id = lax.broadcasted_iota(jnp.int32, shape, 1)

    def block(lc, lr):
        x = f_ref[pl.ds(2 * B * lc + lr, B, stride=2), :]
        ci = (4 * lc + my_col) * B + i_id
        ri = (8 * lr + my_row) * B + t_id
        if lc < 2 and lr == 0:
            dead = (ci >= live) | (ri >= live)
            return jnp.where(dead, jnp.where(ci == ri, 1.0, 0.0), x)
        return jnp.where((ci if lc < 2 else ri) >= live, 0.0, x)

    x0, x1 = block(0, 0), block(1, 0)
    step = (my_col - my_row + 8) % 8
    near = step < 4
    sent = jnp.where(near, x0, x1)
    rest = jnp.where(near, x1, x0)
    on_diagonal = step % 4 == 0
    first_ref[0:B, :] = jnp.where(on_diagonal & (i_id <= t_id), rest, sent)
    first_ref[B : B + 8, :] = jnp.zeros((8, B), F32)
    first_ref[B : B + 1, :] = jnp.sum(
        jnp.where(i_id == t_id, sent, 0.0), axis=0, keepdims=True
    )
    known = y_ref[pl.ds(map_ref[my_group, my_row], 1), :]
    for lc in range(2):
        x = block(lc, 1)
        first_ref[HEAD + lc * B : HEAD + lc * B + B, :] = x
        part = jnp.sum(x * known, axis=1, keepdims=True)
        first_ref[B + 1 + lc : B + 2 + lc, :] = jnp.sum(
            jnp.where(i_id == t_id, part, 0.0), axis=0, keepdims=True
        )
        cols_ref[lc * B : lc * B + B, :] = block(2 + lc, 0)


def chain_kernel(own_ref, other_ref, a_ref, lin_ref, v_ref):
    nb = 8
    m = nb * B
    even = lax.axis_index("row") % 2 == 0
    i_id = lax.broadcasted_iota(jnp.int32, (B, B), 0)
    t_id = lax.broadcasted_iota(jnp.int32, (B, B), 1)
    lower = i_id > t_id

    def rows_of(s, c, lo, hi):
        mine = own_ref[s // 2, c, lo:hi, :]
        theirs = other_ref[s // 2, c, lo:hi, :]
        return jnp.where(even, mine, theirs) if s % 2 == 0 else jnp.where(even, theirs, mine)

    def put(i, j, x):
        a_ref[i * B : i * B + B, j * B : j * B + B] = x

    sums = [None] * nb
    skew = [None] * nb
    for s in range(nb):
        for c in range(4):
            tail = rows_of(s, c, B, B + 8)
            for lc in range(2):
                j = 4 * lc + c
                got = tail[1 + lc : 2 + lc, :]
                sums[j] = got if sums[j] is None else sums[j] + got
            x = rows_of(s, c, 0, B)
            j = c if (c - s) % 8 < 4 else c + 4
            if j == s:
                low = jnp.where(lower, x, 0.0)
                put(s, s, low + low.T + jnp.where(i_id == t_id, tail[0:1, :], 0.0))
                skew[s] = x
            else:
                put(j, s, x)
                put(s, j, x.T)
    for s in range(4):
        z = jnp.where(lower, skew[s + 4].T, skew[s])
        put(s + 4, s, z)
        put(s, s + 4, z.T)
    for j in range(nb):
        v_ref[j : j + 1, :] = sums[j]

    def body(k, carry):
        off = pl.multiple_of(k * B, B)
        rows = factor_block(
            [a_ref[pl.ds(off + G * i, G), pl.ds(off, B)] for i in range(B // G)]
        )
        for i in range(B // G):
            lin_ref[pl.ds(off + G * i, G), :] = rows[i]
        for kk in range(nb - 1):

            @pl.when(k == kk)
            def _():
                s = (kk + 1) * B
                lin = lin_ref[kk * B : s, :]
                w = dot3(lin, a_ref[kk * B : s, s:m], ((1,), (0,)))
                a_ref[kk * B : s, s:m] = w
                low = dot3(a_ref[s:m, kk * B : s], lin, ((1,), (1,)))
                a_ref[s:m, kk * B : s] = low
                a_ref[s:m, s:m] = a_ref[s:m, s:m] - dot3(low, w, ((1,), (0,)))

        return carry

    lax.fori_loop(0, nb, body, 0)


def schur_kernel(a_ref, lin_ref, v_ref, e_ref, c_ref, f_ref, s_ref, t_ref, w_ref):
    nb = 8
    for k in range(nb):
        ks = slice(k * B, k * B + B)
        lc, c = k // 4, k % 4
        e = jnp.concatenate(
            [
                e_ref[c, HEAD + lc * B : HEAD + lc * B + B, :],
                c_ref[k, 0:B, :].T,
                c_ref[k, B : 2 * B, :].T,
                jnp.broadcast_to(v_ref[k : k + 1, :], (B, B)).T,
            ],
            axis=1,
        )
        if k:
            e = e - dot3(a_ref[ks, 0 : k * B], w_ref[0 : k * B, :], ((1,), (0,)))
        w_ref[ks, :] = dot3(lin_ref[ks, :], e, ((1,), (0,)))
    t_ref[...] = w_ref[:, 3 * B :]
    prod = dot3(w_ref[:, B : 3 * B], w_ref[:, 0:B], ((0,), (0,)))
    for b in range(2):
        x = f_ref[pl.ds(2 * B * (2 + b) + 1, B, stride=2), :] - prod[b * B : b * B + B, :]
        for p in range(16):
            s_ref[p, b, :, :] = x[G * p : G * p + G, :]


def sample_kernel(a_ref, lin_ref, t_ref, n_ref, x_ref):
    nb = 8
    xs = [None] * nb
    for k in reversed(range(nb)):
        ks = slice(k * B, k * B + B)
        z = jnp.broadcast_to(n_ref[:, ks], (B, B)).T - t_ref[ks, :]
        if k + 1 < nb:
            acc = None
            for j in range(k + 1, nb):
                term = a_ref[ks, j * B : j * B + B] * xs[j]
                acc = term if acc is None else acc + term
            z = z - jnp.sum(acc, axis=1, keepdims=True)
        xs[k] = jnp.sum(lin_ref[ks, :] * z, axis=0, keepdims=True)
        x_ref[:, ks] = xs[k]


def kernel_call(body, name, outs, scratch, flops, args, smem=()):
    specs = [
        pl.BlockSpec(memory_space=pltpu.SMEM if i in smem else pltpu.VMEM)
        for i in range(len(args))
    ]
    return pl.pallas_call(
        body,
        out_shape=[jax.ShapeDtypeStruct(s, F32) for s in outs],
        in_specs=specs,
        out_specs=[pl.BlockSpec(memory_space=pltpu.VMEM)] * len(outs),
        scratch_shapes=[pltpu.VMEM(s, F32) for s in scratch],
        compiler_params=pltpu.CompilerParams(vmem_limit_bytes=20 * 2**20),
        cost_estimate=pl.CostEstimate(
            flops=flops, bytes_accessed=8 * 2**20, transcendentals=0
        ),
        name=name,
    )(*args)


def local(child_front, top_front, block_map, pivots, noise, top_sample):
    my_row = lax.axis_index("row")
    my_col = lax.axis_index("col")
    front = child_front.reshape(8 * B, B)
    first, cols = kernel_call(
        front_kernel,
        "front",
        [(HEAD + 2 * B, B), (2 * B, B)],
        [],
        10**8,
        (front, block_map, pivots, top_sample.reshape(-1, B)),
        (1, 2),
    )
    wide = lax.all_gather(first, "col")
    own = lax.all_to_all(
        jnp.broadcast_to(wide[:, :HEAD], (4, 4, HEAD, B)),
        "row",
        split_axis=0,
        concat_axis=0,
        axis_index_groups=PARITY,
        tiled=True,
    )
    other = lax.ppermute(own, "row", PAIRS)
    own, other, cols = lax.optimization_barrier((own, other, cols))
    cols_all = lax.all_to_all(
        jnp.broadcast_to(cols, (8, 2 * B, B)), "row", split_axis=0, concat_axis=0, tiled=True
    )
    factor, inverses, coupled = kernel_call(
        chain_kernel,
        "chain",
        [(8 * B, 8 * B), (8 * B, B), (8, B)],
        [],
        4 * 10**9,
        (own, other),
    )
    shares, reduced = kernel_call(
        schur_kernel,
        "schur",
        [(16, 2, G, B), (8 * B, B)],
        [(8 * B, 4 * B)],
        10**9,
        (factor, inverses, coupled, wide, cols_all, front),
    )
    arrived = lax.all_to_all(shares, "group", split_axis=0, concat_axis=0, tiled=True)
    (solved,) = kernel_call(
        sample_kernel,
        "sample",
        [(1, 8 * B)],
        [],
        10**9,
        (factor, inverses, reduced, noise),
    )

    col_blocks = jnp.arange(2, dtype=jnp.int32) * 4 + my_col
    col_target = jnp.take(block_map, col_blocks, axis=1) // 4
    row_target = lax.dynamic_index_in_dim(block_map, my_row, 1, keepdims=False) // 8
    top_cols = top_front.shape[0]
    top_rows = top_front.shape[4]
    col_hot = (
        col_target[:, :, None] == jnp.arange(top_cols, dtype=jnp.int32)[None, None, :]
    ).astype(F32)
    row_hot = (
        row_target[:, None] == jnp.arange(top_rows, dtype=jnp.int32)[None, :]
    ).astype(F32)
    top_tile = top_front.reshape(top_cols, G, top_rows, B)
    placed = row_hot[:, None, None, :, None] * arrived[:, :, :, None, :]
    top_tile = top_tile + jnp.einsum("gak,gamli->kmli", col_hot, placed, precision=HIGH)
    return (top_tile.reshape(top_front.shape), solved)


def solution(mesh):
    return jax.shard_map(
        local,
        mesh=mesh,
        in_specs=(
            P("group", None, "col", None, None, "row", None),
            P(None, "col", "group", None, None, "row", None),
            P(),
            P("group"),
            P("group", None),
            P(),
        ),
        out_specs=(P(None, "col", "group", None, None, "row", None), P("group", None)),
        check_vma=False,
    )
```

time: 180 us -> 133 us (0.74)
  blocking collectives: 84.6 us -> 31.6 us
  local copies, waits for them, and re-layouts: 5.44 us -> 16.1 us
  other arithmetic: 3.52 us -> 0.13 us
  between operations: 3.25 us -> 1.42 us
    all_gather x5 -> x0, blocking collectives: 71.3 us -> none  [the longest x3 43.9 us: local(): lax.all_gather(wide[:, 88 * p:88 * p + 88], 'row', axis_index_groups=PARITY)]
    all_to_all x0 -> x1, blocking collectives: none -> 17.8 us  [local(): lax.all_to_all(jnp.broadcast_to(wide[:, :HEAD], (4, 4, HEAD, B)), 'row',...]
    unnamed x17 -> x28, local copies, waits for them, and re-layouts: 3.02 us -> 14.4 us
    ppermute x4 -> x1, starting transfers between devices: 7.64 us -> 1.91 us  [local(): other = lax.ppermute(own, 'row', PAIRS)]
    all_to_all x0 -> x1, starting transfers between devices: none -> 5.06 us  [local(): lax.all_to_all(jnp.broadcast_to(cols, (8, 2 * B, B)), 'row', split_axis=0...]
    select_n x1 -> x0, other arithmetic: 2.88 us -> none  [local(): tile = jnp.where(dead, unit, tile)]
    all_to_all x1, waiting for transfers between devices: 13.2 us -> 10.9 us  [local(): lax.all_to_all(shares, 'group', split_axis=0, concat_axis=0, tiled=True)]
    pallas_call x1 -> x4, Pallas kernels: 47.8 us -> 47.9 us  [kernel_call(): pl.pallas_call(body, out_shape=[jax.ShapeDtypeStruct(s, F32) for s in out...]
  transfers between devices with their start and end apart: 5 -> 3, of which waited for: 1 -> 2; matrix products, arithmetic and copies ran while one was open for 0% -> 1% of each run, Pallas kernels for 0% -> 32%
where the time goes in v2:
time: 133 us; the launch traced here: 132 us
  Pallas kernels  47.9 us (36%)
  blocking collectives  31.6 us (24%)
  starting transfers between devices  21.9 us (16%)
  local copies, waits for them, and re-layouts  16.1 us (12%)
  waiting for transfers between devices  12.6 us (9%)
  between operations  1.42 us (1%)
    pallas_call x4, Pallas kernels, kernel_call(): pl.pallas_call(body, out_shape=[jax.ShapeDtypeStruct(s, F32) for s in out...  47.9 us
    all_to_all x1, blocking collectives, local(): lax.all_to_all(jnp.broadcast_to(wide[:, :HEAD], (4, 4, HEAD, B)), 'row',...  17.8 us
    all_to_all x1, starting transfers between devices, local(): lax.all_to_all(shares, 'group', split_axis=0, concat_axis=0, tiled=True)  14.9 us
    unnamed x28, local copies, waits for them, and re-layouts  14.4 us
    all_gather x1, blocking collectives, local(): wide = lax.all_gather(first, 'col')  13.9 us
    all_to_all x1, waiting for transfers between devices, local(): lax.all_to_all(shares, 'group', split_axis=0, concat_axis=0, tiled=True)  10.9 us
    all_to_all x1, starting transfers between devices, local(): lax.all_to_all(jnp.broadcast_to(cols, (8, 2 * B, B)), 'row', split_axis=0...  5.06 us
  transfers between devices with their start and end apart: 3, of which 2 were waited for; matrix products, arithmetic and copies ran while one was open for 1% of the time, Pallas kernels for 32%

profile of v2, /device:TPU:2, one launch (start us, length us, event | category | flops | bytes accessed | tf_op | source)
XLA Modules:
  0.0 132.2 jit_solution(4428547841512934495)
XLA Ops:
  0.6 0.8 copy.9.map_ref
  2.0 0.0 copy-start.3
  2.1 1.0 copy-done.3
  3.1 0.0 copy-start.7
  3.1 0.7 copy-done.7
  3.8 0.8 front.1
  4.6 13.9 %all-gather = f32[1568,128]{1,0:T(8,128)S(1)} all-gather(f32[392,128]{1,0:T(8,128)S(1)} %get-tuple-element.12), channel_id=2, replica_groups=mesh['group'=16,'row'=8,'col'=4] {'col'}, dimensions={0}, use_global_device_ids=true | all-gather | bytes 1003520 | tf_op jit(solution)/shard_map/all_gather | solution.py:249
  18.5 0.1 broadcast_in_dim.24
  18.6 17.8 %all_to_all.15.own_ref = f32[4,4,136,128]{3,2,1,0:T(8,128)S(1)} all-to-all(f32[4,4,136,128]{3,2,1,0:T(8,128)S(1)} %broadcast_in_dim.24), channel_id=1, replica_groups={{0,8,16,24},{4,12,20,28},{1,9,17,25},{5,13,21,29},{2,10,18,26},{6,14,22..., dimensions={0} | all-to-all | bytes 2228224 | tf_op jit(solution)/shard_map/all_to_all | solution.py:250
  36.4 1.9 %collective-permute-start = (f32[4,4,136,128]{3,2,1,0:T(8,128)S(1)}, f32[4,4,136,128]{3,2,1,0:T(8,128)S(1)}, u32[]{:S(2)}, u32[]{:S(2)}) collective-permute-start(f32[4,4,136,128]{3,2,1,0:T(8,128)S(1)} %all_to_all.15.own_ref), channel_id=1, source_target_pairs={{0,4},{4,0},{8,12},{12,8},{16,20},{20,16},{24,28},{28,24},{1,5},{5... | collective-permute-start | bytes 3342344 | tf_op jit(solution)/shard_map/ppermute | solution.py:258
  38.3 0.0 copy-start.5
  38.3 1.0 copy-done.5
  39.3 1.7 %collective-permute-done.other_ref = f32[4,4,136,128]{3,2,1,0:T(8,128)S(1)} collective-permute-done((f32[4,4,136,128]{3,2,1,0:T(8,128)S(1)}, f32[4,4,136,128]{3,2,1,0:T(8,128)S(1)}, u32[]{:S(2)}, u32[]{:S(2)}) %collective-permute-start) | collective-permute-done | bytes 1114144 | tf_op jit(solution)/shard_map/ppermute | solution.py:258
  41.0 0.0 copy-start.9
  41.0 1.0 copy-done.9
  42.0 1.0 broadcast_in_dim.25
  43.0 0.0 copy-start.11
  43.0 5.1 %all-to-all-start.1 = ((f32[8,256,128]{2,1,0:T(8,128)}), f32[8,256,128]{2,1,0:T(8,128)S(1)}, u32[]{:S(2)}, u32[]{:S(2)}) async-start(f32[8,256,128]{2,1,0:T(8,128)} %broadcast_in_dim.25), calls=%async_computation.1 | async-start | bytes 2097152 | tf_op jit(solution)/shard_map/all_to_all | solution.py:260
  48.1 0.0 copy-done.11
  48.1 0.6 gather_fusion
  48.7 0.0 copy-start.6
  48.7 1.2 copy-done.6
  50.0 0.0 copy-start.10
  50.0 1.2 copy-done.10
  51.2 0.0 copy-start.4
  51.2 40.2 %chain.1 = (f32[1024,1024]{1,0:T(8,128)S(1)}, f32[1024,128]{1,0:T(8,128)S(1)}, f32[8,128]{1,0:T(8,128)S(1)}) custom-call(f32[4,4,136,128]{3,2,1,0:T(8,128)S(1)} %copy-done.6, f32[4,4,136,128]{3,2,1,0:T(8,128)S(1)} %copy-done.10), custom_call_target="tpu_custom_call" | custom-call | flops 4000000000 | bytes 8388608 | tf_op jit(solution)/shard_map/chain/pallas_call | solution.py:222
  91.5 0.0 copy-start
  91.5 1.9 %copy-done = f32[1024,1024]{1,0:T(8,128)} copy-done((f32[1024,1024]{1,0:T(8,128)}, f32[1024,1024]{1,0:T(8,128)S(1)}, u32[]{:S(2)}) %copy-start) | copy-done | bytes 4194328
  93.4 0.0 all-to-all-done.1.c_ref
  93.4 0.0 copy-done.4
  93.4 0.0 copy-start.1
  93.4 2.2 %copy-done.1 = f32[1024,1024]{1,0:T(8,128)S(1)} copy-done((f32[1024,1024]{1,0:T(8,128)S(1)}, f32[1024,1024]{1,0:T(8,128)}, u32[]{:S(2)}) %copy-start.1) | copy-done | bytes 4194328
  95.6 0.0 copy-start.8
  95.6 5.3 %schur.1 = (f32[16,2,8,128]{3,2,1,0:T(8,128)}, f32[1024,128]{1,0:T(8,128)S(1)}) custom-call(f32[1024,1024]{1,0:T(8,128)S(1)} %copy-done.1, f32[1024,128]{1,0:T(8,128)S(1)} %get-tuple-element.17.lin_ref, f32[8,128]{1,0:T(8,128)S(1)} %get-tuple-element.18.v_ref, f32[4,392,128]{2,1,0:T(8,128)S(1)} %bitcast.32, f32[8,256,128]{2,1,0:T(8,128)S(1)} %all-to-all-done.1.c_ref, ...), custom_call_target="tpu_custom_call" | custom-call | flops 1000000000 | bytes 8388608 | tf_op jit(solution)/shard_map/schur/pallas_call | solution.py:222
  100.9 14.9 %all-to-all-start.2 = ((f32[16,2,8,128]{3,2,1,0:T(8,128)}), f32[16,2,8,128]{3,2,1,0:T(8,128)S(1)}, u32[]{:S(2)}, u32[]{:S(2)}) async-start(f32[16,2,8,128]{3,2,1,0:T(8,128)} %get-tuple-element.20), calls=%async_computation.2 | async-start | bytes 262144 | tf_op jit(solution)/shard_map/all_to_all | solution.py:279
  115.9 0.1 and_select_fusion.1
  116.0 0.0 copy-done.8
  116.0 0.0 copy-start.2
  116.0 2.2 %copy-done.2 = f32[1024,1024]{1,0:T(8,128)S(1)} copy-done((f32[1024,1024]{1,0:T(8,128)S(1)}, f32[1024,1024]{1,0:T(8,128)}, u32[]{:S(2)}) %copy-start.2) | copy-done | bytes 4194328
  118.2 0.0 copy-start.12
  118.2 1.5 %sample.1 = f32[1,1024]{1,0:T(1,128)} custom-call(f32[1024,1024]{1,0:T(8,128)S(1)} %copy-done.2, f32[1024,128]{1,0:T(8,128)S(1)} %get-tuple-element.17.lin_ref, f32[1024,128]{1,0:T(8,128)S(1)} %get-tuple-element.21.t_ref, f32[1,1024]{1,0:T(1,128)S(1)} %copy-done.8), custom_call_target="tpu_custom_call" | custom-call | flops 1000000000 | bytes 8388608 | tf_op jit(solution)/shard_map/sample/pallas_call | solution.py:222
  119.7 10.9 %all-to-all-done.2 = f32[16,2,8,128]{3,2,1,0:T(8,128)S(1)} async-done(((f32[16,2,8,128]{3,2,1,0:T(8,128)}), f32[16,2,8,128]{3,2,1,0:T(8,128)S(1)}, u32[]{:S(2)}, u32[]{:S(2)}) %all-to-all-start.2) | async-done | bytes 131104 | tf_op jit(solution)/shard_map/all_to_all | solution.py:279
  130.6 0.0 copy-done.12
  130.7 0.5 fusion.1
  131.2 1.0 copy.11
  (7 shorter events, 0.1 us)
Async XLA Ops:
  2.0 1.0 copy-start.3
  3.1 0.7 copy-start.7
  36.4 4.6 %collective-permute-start = (f32[4,4,136,128]{3,2,1,0:T(8,128)S(1)}, f32[4,4,136,128]{3,2,1,0:T(8,128)S(1)}, u32[]{:S(2)}, u32[]{:S(2)}) collective-permute-start(f32[4,4,136,128]{3,2,1,0:T(8,128)S(1)} %all_to_all.15.own_ref), channel_id=1, source_target_pairs={{0,4},{4,0},{8,12},{12,8},{16,20},{20,16},{24,28},{28,24},{1,5},{5... | collective-permute-start | bytes 3342344 | tf_op jit(solution)/shard_map/ppermute | solution.py:258
  38.3 1.0 copy-start.5
  41.0 1.0 copy-start.9
  43.0 5.1 %copy-start.11 = (s32[16,8]{0,1:T(8,128)S(1)}, s32[16,8]{0,1:T(8,128)}, u32[]{:S(2)}) copy-start(s32[16,8]{0,1:T(8,128)} %param.8) | copy-start | bytes 1540
  43.0 50.4 %all-to-all-start.1 = ((f32[8,256,128]{2,1,0:T(8,128)}), f32[8,256,128]{2,1,0:T(8,128)S(1)}, u32[]{:S(2)}, u32[]{:S(2)}) async-start(f32[8,256,128]{2,1,0:T(8,128)} %broadcast_in_dim.25), calls=%async_computation.1 | async-start | bytes 2097152 | tf_op jit(solution)/shard_map/all_to_all | solution.py:260
  48.7 1.2 copy-start.6
  50.0 1.2 copy-start.10
  51.2 42.2 %copy-start.4 = (f32[1,4,1,128,2,1,128]{6,5,4,3,2,1,0:T(1,128)S(1)}, f32[1,4,1,128,2,1,128]{6,5,4,3,2,1,0:T(1,128)}, u32[]{:S(2)}) copy-start(f32[1,4,1,128,2,1,128]{6,5,4,3,2,1,0:T(1,128)} %param.6) | copy-start | bytes 1572868
  91.5 1.9 %copy-start = (f32[1024,1024]{1,0:T(8,128)}, f32[1024,1024]{1,0:T(8,128)S(1)}, u32[]{:S(2)}) copy-start(f32[1024,1024]{1,0:T(8,128)S(1)} %get-tuple-element.16.a_ref) | copy-start | bytes 12582916
  93.4 2.2 %copy-start.1 = (f32[1024,1024]{1,0:T(8,128)S(1)}, f32[1024,1024]{1,0:T(8,128)}, u32[]{:S(2)}) copy-start(f32[1024,1024]{1,0:T(8,128)} %copy-done) | copy-start | bytes 12582916
  95.6 20.4 %copy-start.8 = (f32[1,1024]{1,0:T(1,128)S(1)}, f32[1,1024]{1,0:T(1,128)}, u32[]{:S(2)}) copy-start(f32[1,1024]{1,0:T(1,128)} %n_ref.1) | copy-start | bytes 12292
  100.9 29.7 %all-to-all-start.2 = ((f32[16,2,8,128]{3,2,1,0:T(8,128)}), f32[16,2,8,128]{3,2,1,0:T(8,128)S(1)}, u32[]{:S(2)}, u32[]{:S(2)}) async-start(f32[16,2,8,128]{3,2,1,0:T(8,128)} %get-tuple-element.20), calls=%async_computation.2 | async-start | bytes 262144 | tf_op jit(solution)/shard_map/all_to_all | solution.py:279
  116.0 2.2 %copy-start.2 = (f32[1024,1024]{1,0:T(8,128)S(1)}, f32[1024,1024]{1,0:T(8,128)}, u32[]{:S(2)}) copy-start(f32[1024,1024]{1,0:T(8,128)} %copy-done) | copy-start | bytes 12582916
  118.2 12.5 %copy-start.12 = (f32[12,1,1,8,6,1,128]{6,5,4,3,2,1,0:T(1,128)S(1)}, f32[12,1,1,8,6,1,128]{6,5,4,3,2,1,0:T(1,128)}, u32[]{:S(2)}) copy-start(f32[12,1,1,8,6,1,128]{6,5,4,3,2,1,0:T(1,128)} %param.7) | copy-start | bytes 884740

commit v3 on v2

--- a/solution.py
+++ b/solution.py
@@ -25,11 +25,17 @@
 def dot3(left, right, dims):
     lh, ll = halves(left)
     rh, rl = halves(right)
-
-    def part(p, q):
-        return lax.dot_general(p, q, (dims, ((), ())), preferred_element_type=F32)
-
-    return part(lh, rh) + (part(lh, rl) + part(ll, rh))
+    (ld,), (rd,) = dims
+    return lax.dot_general(
+        jnp.concatenate([lh, ll, lh], axis=ld),
+        jnp.concatenate([rh, rh, rl], axis=rd),
+        (dims, ((), ())),
+        preferred_element_type=F32,
+    )
+
+
+def spread(x, j):
+    return jnp.broadcast_to(x[j : j + 1, :], (G, B))
 
 
 def factor_block(vs):
@@ -44,19 +50,24 @@
         cols = {}
         for v in range(g, n):
             for c in range(G):
-                cols[v, c] = jnp.broadcast_to(vs[v][:, base + c : base + c + 1], (G, B))
+                cols[v, c] = jnp.take_along_axis(
+                    vs[v],
+                    jnp.full((G, B), base + c, jnp.int32),
+                    axis=1,
+                    mode="promise_in_bounds",
+                )
         vs[g] = jnp.where(ingroup, jnp.where(lane - base == sub, 1.0, 0.0), vs[g])
         for v in range(g + 1, n):
             vs[v] = jnp.where(ingroup, 0.0, vs[v])
         dvec = jnp.ones((G, B), F32)
+        d = spread(cols[g, 0], 0)
         for j in range(G):
-            d = jnp.broadcast_to(cols[g, j][j : j + 1, :], (G, B))
             r = 1.0 / d
             dvec = jnp.where(sub == j, d, dvec)
-            us = [
-                jnp.broadcast_to(cols[g, c][j : j + 1, :], (G, B)) for c in range(j + 1, G)
-            ]
-            row = jnp.broadcast_to(vs[g][j : j + 1, :], (G, B))
+            us = [spread(cols[g, c], j) for c in range(j + 1, G)]
+            row = spread(vs[g], j)
+            if j + 1 < G:
+                d = spread(cols[g, j + 1], j + 1) - spread(cols[g, j], j + 1) * us[0] * r
             for v in range(g, n):
                 f = cols[v, j] * r
                 if v == g:
@@ -108,7 +119,7 @@
         cols_ref[lc * B : lc * B + B, :] = block(2 + lc, 0)
 
 
-def chain_kernel(own_ref, other_ref, a_ref, lin_ref, v_ref):
+def chain_kernel(own_ref, other_ref, fac_ref, lin_ref, v_ref, a_ref, sems):
     nb = 8
     m = nb * B
     even = lax.axis_index("row") % 2 == 0
@@ -149,6 +160,10 @@
     for j in range(nb):
         v_ref[j : j + 1, :] = sums[j]
 
+    def row_copy(off, k):
+        rows = pl.ds(off, B)
+        return pltpu.make_async_copy(a_ref.at[rows, :], fac_ref.at[rows, :], sems.at[k])
+
     def body(k, carry):
         off = pl.multiple_of(k * B, B)
         rows = factor_block(
@@ -168,13 +183,23 @@
                 a_ref[s:m, kk * B : s] = low
                 a_ref[s:m, s:m] = a_ref[s:m, s:m] - dot3(low, w, ((1,), (0,)))
 
+        row_copy(off, k).start()
         return carry
 
     lax.fori_loop(0, nb, body, 0)
-
-
-def schur_kernel(a_ref, lin_ref, v_ref, e_ref, c_ref, f_ref, s_ref, t_ref, w_ref):
+    for k in range(nb):
+        row_copy(k * B, k).wait()
+
+
+def schur_kernel(
+    fac_ref, lin_ref, v_ref, e_ref, c_ref, f_ref, s_ref, t_ref, w_ref, a_ref, sems
+):
     nb = 8
+    copies = [None]
+    for k in range(1, nb):
+        part = (pl.ds(k * B, B), pl.ds(0, k * B))
+        copies.append(pltpu.make_async_copy(fac_ref.at[part], a_ref.at[part], sems.at[k]))
+        copies[k].start()
     for k in range(nb):
         ks = slice(k * B, k * B + B)
         lc, c = k // 4, k % 4
@@ -188,6 +213,7 @@
             axis=1,
         )
         if k:
+            copies[k].wait()
             e = e - dot3(a_ref[ks, 0 : k * B], w_ref[0 : k * B, :], ((1,), (0,)))
         w_ref[ks, :] = dot3(lin_ref[ks, :], e, ((1,), (0,)))
     t_ref[...] = w_ref[:, 3 * B :]
@@ -198,13 +224,19 @@
             s_ref[p, b, :, :] = x[G * p : G * p + G, :]
 
 
-def sample_kernel(a_ref, lin_ref, t_ref, n_ref, x_ref):
+def sample_kernel(fac_ref, lin_ref, t_ref, n_ref, x_ref, a_ref, sems):
     nb = 8
+    copies = {}
+    for k in reversed(range(nb - 1)):
+        part = (pl.ds(k * B, B), pl.ds((k + 1) * B, (nb - 1 - k) * B))
+        copies[k] = pltpu.make_async_copy(fac_ref.at[part], a_ref.at[part], sems.at[k])
+        copies[k].start()
     xs = [None] * nb
     for k in reversed(range(nb)):
         ks = slice(k * B, k * B + B)
         z = jnp.broadcast_to(n_ref[:, ks], (B, B)).T - t_ref[ks, :]
         if k + 1 < nb:
+            copies[k].wait()
             acc = None
             for j in range(k + 1, nb):
                 term = a_ref[ks, j * B : j * B + B] * xs[j]
@@ -214,18 +246,25 @@
         x_ref[:, ks] = xs[k]
 
 
-def kernel_call(body, name, outs, scratch, flops, args, smem=()):
-    specs = [
-        pl.BlockSpec(memory_space=pltpu.SMEM if i in smem else pltpu.VMEM)
+def kernel_call(body, name, outs, scratch, flops, args, smem=(), away=(), away_out=(), copies=0):
+    def spec(space):
+        return pl.BlockSpec(memory_space=space)
+
+    ins = [
+        spec(pltpu.SMEM if i in smem else pltpu.HBM if i in away else pltpu.VMEM)
         for i in range(len(args))
     ]
+    results = [spec(pltpu.HBM if i in away_out else pltpu.VMEM) for i in range(len(outs))]
+    scratch = [pltpu.VMEM(s, F32) for s in scratch]
+    if copies:
+        scratch.append(pltpu.SemaphoreType.DMA((copies,)))
     return pl.pallas_call(
         body,
         out_shape=[jax.ShapeDtypeStruct(s, F32) for s in outs],
-        in_specs=specs,
-        out_specs=[pl.BlockSpec(memory_space=pltpu.VMEM)] * len(outs),
-        scratch_shapes=[pltpu.VMEM(s, F32) for s in scratch],
-        compiler_params=pltpu.CompilerParams(vmem_limit_bytes=20 * 2**20),
+        in_specs=ins,
+        out_specs=results,
+        scratch_shapes=scratch,
+        compiler_params=pltpu.CompilerParams(vmem_limit_bytes=(60 if copies else 20) * 2**20),
         cost_estimate=pl.CostEstimate(
             flops=flops, bytes_accessed=8 * 2**20, transcendentals=0
         ),
@@ -256,7 +295,7 @@
         tiled=True,
     )
     other = lax.ppermute(own, "row", PAIRS)
-    own, other, cols = lax.optimization_barrier((own, other, cols))
+    cols, _ = lax.optimization_barrier((cols, other[0, 0, 0:8, :]))
     cols_all = lax.all_to_all(
         jnp.broadcast_to(cols, (8, 2 * B, B)), "row", split_axis=0, concat_axis=0, tiled=True
     )
@@ -264,26 +303,32 @@
         chain_kernel,
         "chain",
         [(8 * B, 8 * B), (8 * B, B), (8, B)],
-        [],
+        [(8 * B, 8 * B)],
         4 * 10**9,
         (own, other),
+        away_out=(0,),
+        copies=8,
     )
     shares, reduced = kernel_call(
         schur_kernel,
         "schur",
         [(16, 2, G, B), (8 * B, B)],
-        [(8 * B, 4 * B)],
+        [(8 * B, 4 * B), (8 * B, 8 * B)],
         10**9,
         (factor, inverses, coupled, wide, cols_all, front),
+        away=(0,),
+        copies=8,
     )
     arrived = lax.all_to_all(shares, "group", split_axis=0, concat_axis=0, tiled=True)
     (solved,) = kernel_call(
         sample_kernel,
         "sample",
         [(1, 8 * B)],
-        [],
+        [(8 * B, 8 * B)],
         10**9,
         (factor, inverses, reduced, noise),
+        away=(0,),
+        copies=8,
     )
 
     col_blocks = jnp.arange(2, dtype=jnp.int32) * 4 + my_col

time: 133 us -> 119 us (0.89)
  local copies, waits for them, and re-layouts: 16.1 us -> 7.28 us
  Pallas kernels: 47.9 us -> 44.1 us
  waiting for transfers between devices: 12.6 us -> 10.9 us
    unnamed x28 -> x18, local copies, waits for them, and re-layouts: 14.4 us -> 5.55 us
    pallas_call x4, Pallas kernels: 47.9 us -> 44.1 us  [kernel_call(): pl.pallas_call(body, out_shape=[jax.ShapeDtypeStruct(s, F32) for s in out...]
    ppermute x1, waiting for transfers between devices: 1.71 us -> 0.01 us  [local(): other = lax.ppermute(own, 'row', PAIRS)]
  transfers between devices with their start and end apart: 3 -> 3, of which waited for: 2 -> 1; matrix products, arithmetic and copies ran while one was open for 1% -> 1% of each run, Pallas kernels for 32% -> 30%
where the time goes in v3:
time: 119 us; the launch traced here: 118 us
  Pallas kernels  44.1 us (37%)
  blocking collectives  31.6 us (27%)
  starting transfers between devices  21.9 us (18%)
  waiting for transfers between devices  10.9 us (9%)
  local copies, waits for them, and re-layouts  7.28 us (6%)
  between operations  1.43 us (1%)
    pallas_call x4, Pallas kernels, kernel_call(): pl.pallas_call(body, out_shape=[jax.ShapeDtypeStruct(s, F32) for s in out...  44.1 us
    all_to_all x1, blocking collectives, local(): lax.all_to_all(jnp.broadcast_to(wide[:, :HEAD], (4, 4, HEAD, B)), 'row',...  17.8 us
    all_to_all x1, starting transfers between devices, local(): lax.all_to_all(shares, 'group', split_axis=0, concat_axis=0, tiled=True)  15 us
    all_gather x1, blocking collectives, local(): wide = lax.all_gather(first, 'col')  13.9 us
    all_to_all x1, waiting for transfers between devices, local(): lax.all_to_all(shares, 'group', split_axis=0, concat_axis=0, tiled=True)  10.9 us
    unnamed x18, local copies, waits for them, and re-layouts  5.55 us
    all_to_all x1, starting transfers between devices, local(): lax.all_to_all(jnp.broadcast_to(cols, (8, 2 * B, B)), 'row', split_axis=0...  5.06 us
  transfers between devices with their start and end apart: 3, of which 1 were waited for; matrix products, arithmetic and copies ran while one was open for 1% of the time, Pallas kernels for 30%

profile of v3, /device:TPU:2, one launch (start us, length us, event | category | flops | bytes accessed | tf_op | source)
XLA Modules:
  0.0 117.9 jit_solution(4693185257652563389)
XLA Ops:
  0.6 0.8 copy.9.map_ref
  2.0 0.0 copy-start
  2.1 1.0 copy-done
  3.1 0.0 copy-start.1
  3.1 0.7 copy-done.1
  3.8 0.8 front.1
  4.6 13.9 %all-gather = f32[1568,128]{1,0:T(8,128)S(1)} all-gather(f32[392,128]{1,0:T(8,128)S(1)} %get-tuple-element.9), channel_id=2, replica_groups=mesh['group'=16,'row'=8,'col'=4] {'col'}, dimensions={0}, use_global_device_ids=true | all-gather | bytes 1003520 | tf_op jit(solution)/shard_map/all_gather | solution.py:288
  18.5 0.0 copy-start.2
  18.5 0.1 broadcast_in_dim.24
  18.6 17.8 %all_to_all.15.own_ref = f32[4,4,136,128]{3,2,1,0:T(8,128)S(1)} all-to-all(f32[4,4,136,128]{3,2,1,0:T(8,128)S(1)} %broadcast_in_dim.24), channel_id=1, replica_groups={{0,8,16,24},{4,12,20,28},{1,9,17,25},{5,13,21,29},{2,10,18,26},{6,14,22..., dimensions={0} | all-to-all | bytes 2228224 | tf_op jit(solution)/shard_map/all_to_all | solution.py:289
  36.4 0.0 copy-done.2
  36.4 0.0 copy-start.5
  36.4 1.9 %collective-permute-start = (f32[4,4,136,128]{3,2,1,0:T(8,128)S(1)}, f32[4,4,136,128]{3,2,1,0:T(8,128)S(1)}, u32[]{:S(2)}, u32[]{:S(2)}) collective-permute-start(f32[4,4,136,128]{3,2,1,0:T(8,128)S(1)} %all_to_all.15.own_ref), channel_id=1, source_target_pairs={{0,4},{4,0},{8,12},{12,8},{16,20},{20,16},{24,28},{28,24},{1,5},{5... | collective-permute-start | bytes 3342344 | tf_op jit(solution)/shard_map/ppermute | solution.py:297
  38.3 1.0 broadcast_in_dim.25
  39.3 0.0 copy-start.4
  39.3 0.0 copy-done.5
  39.3 5.1 %all-to-all-start.1 = ((f32[8,256,128]{2,1,0:T(8,128)}), f32[8,256,128]{2,1,0:T(8,128)S(1)}, u32[]{:S(2)}, u32[]{:S(2)}) async-start(f32[8,256,128]{2,1,0:T(8,128)} %broadcast_in_dim.25), calls=%async_computation.1 | async-start | bytes 2097152 | tf_op jit(solution)/shard_map/all_to_all | solution.py:299
  44.4 0.0 copy-done.4
  44.4 0.6 gather_fusion
  45.0 0.0 collective-permute-done.other_ref
  45.0 0.0 copy-start.7
  45.0 1.0 copy-done.7
  46.0 31.5 %chain.1 = (f32[1024,1024]{1,0:T(8,128)}, f32[1024,128]{1,0:T(8,128)}, f32[8,128]{1,0:T(8,128)}) custom-call(f32[4,4,136,128]{3,2,1,0:T(8,128)} %copy-done.5, f32[4,4,136,128]{3,2,1,0:T(8,128)} %copy-done.7), custom_call_target="tpu_custom_call" | custom-call | flops 4000000000 | bytes 8388608 | tf_op jit(solution)/shard_map/chain/pallas_call | solution.py:261
  77.5 0.0 all-to-all-done.1.c_ref
  77.5 0.0 copy-start.3
  77.5 1.0 copy-done.3
  78.5 8.1 %schur.1 = (f32[16,2,8,128]{3,2,1,0:T(8,128)}, f32[1024,128]{1,0:T(8,128)}) custom-call(f32[1024,1024]{1,0:T(8,128)} %get-tuple-element.10.fac_ref, f32[1024,128]{1,0:T(8,128)} %get-tuple-element.11.lin_ref, f32[8,128]{1,0:T(8,128)} %get-tuple-element.12.v_ref, f32[4,392,128]{2,1,0:T(8,128)} %bitcast.35, f32[8,256,128]{2,1,0:T(8,128)} %copy-done.3, ...), custom_call_target="tpu_custom_call" | custom-call | flops 1000000000 | bytes 8388608 | tf_op jit(solution)/shard_map/schur/pallas_call | solution.py:261
  86.7 15.0 %all-to-all-start.2 = ((f32[16,2,8,128]{3,2,1,0:T(8,128)}), f32[16,2,8,128]{3,2,1,0:T(8,128)S(1)}, u32[]{:S(2)}, u32[]{:S(2)}) async-start(f32[16,2,8,128]{3,2,1,0:T(8,128)} %get-tuple-element.14), calls=%async_computation.2 | async-start | bytes 262144 | tf_op jit(solution)/shard_map/all_to_all | solution.py:322
  101.6 0.1 and_select_fusion.1
  101.7 0.0 copy-start.6
  101.7 3.7 %sample.1 = f32[1,1024]{1,0:T(1,128)} custom-call(f32[1024,1024]{1,0:T(8,128)} %get-tuple-element.10.fac_ref, f32[1024,128]{1,0:T(8,128)} %get-tuple-element.11.lin_ref, f32[1024,128]{1,0:T(8,128)} %get-tuple-element.15.t_ref, f32[1,1024]{1,0:T(1,128)} %n_ref.1), custom_call_target="tpu_custom_call" | custom-call | flops 1000000000 | bytes 8388608 | tf_op jit(solution)/shard_map/sample/pallas_call | solution.py:261
  105.5 10.9 %all-to-all-done.2 = f32[16,2,8,128]{3,2,1,0:T(8,128)S(1)} async-done(((f32[16,2,8,128]{3,2,1,0:T(8,128)}), f32[16,2,8,128]{3,2,1,0:T(8,128)S(1)}, u32[]{:S(2)}, u32[]{:S(2)}) %all-to-all-start.2) | async-done | bytes 131104 | tf_op jit(solution)/shard_map/all_to_all | solution.py:322
  116.4 0.0 copy-done.6
  116.4 0.5 fusion.1
  116.9 1.0 copy.11
  (7 shorter events, 0.1 us)
Async XLA Ops:
  2.0 1.0 copy-start
  3.1 0.7 copy-start.1
  18.5 17.9 %copy-start.2 = (f32[1568,128]{1,0:T(8,128)}, f32[1568,128]{1,0:T(8,128)S(1)}, u32[]{:S(2)}) copy-start(f32[1568,128]{1,0:T(8,128)S(1)} %all-gather) | copy-start | bytes 2408452
  36.4 3.0 %copy-start.5 = (f32[4,4,136,128]{3,2,1,0:T(8,128)}, f32[4,4,136,128]{3,2,1,0:T(8,128)S(1)}, u32[]{:S(2)}) copy-start(f32[4,4,136,128]{3,2,1,0:T(8,128)S(1)} %all_to_all.15.own_ref) | copy-start | bytes 3342340
  36.4 8.6 %collective-permute-start = (f32[4,4,136,128]{3,2,1,0:T(8,128)S(1)}, f32[4,4,136,128]{3,2,1,0:T(8,128)S(1)}, u32[]{:S(2)}, u32[]{:S(2)}) collective-permute-start(f32[4,4,136,128]{3,2,1,0:T(8,128)S(1)} %all_to_all.15.own_ref), channel_id=1, source_target_pairs={{0,4},{4,0},{8,12},{12,8},{16,20},{20,16},{24,28},{28,24},{1,5},{5... | collective-permute-start | bytes 3342344 | tf_op jit(solution)/shard_map/ppermute | solution.py:297
  39.3 5.1 %copy-start.4 = (s32[16,8]{0,1:T(8,128)S(1)}, s32[16,8]{0,1:T(8,128)}, u32[]{:S(2)}) copy-start(s32[16,8]{0,1:T(8,128)} %param.8) | copy-start | bytes 1540
  39.3 38.2 %all-to-all-start.1 = ((f32[8,256,128]{2,1,0:T(8,128)}), f32[8,256,128]{2,1,0:T(8,128)S(1)}, u32[]{:S(2)}, u32[]{:S(2)}) async-start(f32[8,256,128]{2,1,0:T(8,128)} %broadcast_in_dim.25), calls=%async_computation.1 | async-start | bytes 2097152 | tf_op jit(solution)/shard_map/all_to_all | solution.py:299
  45.0 1.0 copy-start.7
  77.5 1.0 copy-start.3
  86.7 29.7 %all-to-all-start.2 = ((f32[16,2,8,128]{3,2,1,0:T(8,128)}), f32[16,2,8,128]{3,2,1,0:T(8,128)S(1)}, u32[]{:S(2)}, u32[]{:S(2)}) async-start(f32[16,2,8,128]{3,2,1,0:T(8,128)} %get-tuple-element.14), calls=%async_computation.2 | async-start | bytes 262144 | tf_op jit(solution)/shard_map/all_to_all | solution.py:322
  101.7 14.7 %copy-start.6 = (f32[12,1,1,8,6,1,128]{6,5,4,3,2,1,0:T(1,128)S(1)}, f32[12,1,1,8,6,1,128]{6,5,4,3,2,1,0:T(1,128)}, u32[]{:S(2)}) copy-start(f32[12,1,1,8,6,1,128]{6,5,4,3,2,1,0:T(1,128)} %param.7) | copy-start | bytes 884740

commit v4 on v3

--- a/solution.py
+++ b/solution.py
@@ -40,43 +40,63 @@
 
 def factor_block(vs):
     n = len(vs)
+    pair, panel = 2, 8
+    width = pair * G
     sub = lax.broadcasted_iota(jnp.int32, (G, B), 0)
     lane = lax.broadcasted_iota(jnp.int32, (G, B), 1)
     vs = list(vs)
-    out = []
-    for g in range(n):
-        base = g * G
-        ingroup = (lane >= base) & (lane < base + G)
-        cols = {}
-        for v in range(g, n):
-            for c in range(G):
-                cols[v, c] = jnp.take_along_axis(
-                    vs[v],
-                    jnp.full((G, B), base + c, jnp.int32),
-                    axis=1,
-                    mode="promise_in_bounds",
-                )
-        vs[g] = jnp.where(ingroup, jnp.where(lane - base == sub, 1.0, 0.0), vs[g])
-        for v in range(g + 1, n):
-            vs[v] = jnp.where(ingroup, 0.0, vs[v])
-        dvec = jnp.ones((G, B), F32)
-        d = spread(cols[g, 0], 0)
-        for j in range(G):
-            r = 1.0 / d
-            dvec = jnp.where(sub == j, d, dvec)
-            us = [spread(cols[g, c], j) for c in range(j + 1, G)]
-            row = spread(vs[g], j)
-            if j + 1 < G:
-                d = spread(cols[g, j + 1], j + 1) - spread(cols[g, j], j + 1) * us[0] * r
-            for v in range(g, n):
-                f = cols[v, j] * r
-                if v == g:
-                    f = jnp.where(sub > j, f, 0.0)
-                for i, c in enumerate(range(j + 1, G)):
-                    cols[v, c] = cols[v, c] - f * us[i]
-                vs[v] = vs[v] - f * row
-        out.append(jnp.where(lane - base <= sub, vs[g] * lax.rsqrt(dvec), 0.0))
-    return out
+    dvec = [jnp.ones((G, B), F32)] * n
+    rvec = [jnp.ones((G, B), F32)] * n
+    for p0 in range(0, n, panel):
+        p1 = p0 + panel
+        for g in range(p0, p1, pair):
+            base = g * G
+            ingroup = (lane >= base) & (lane < base + width)
+            cols = {}
+            for v in range(g, p1):
+                for c in range(width):
+                    cols[v, c] = jnp.take_along_axis(
+                        vs[v],
+                        jnp.full((G, B), base + c, jnp.int32),
+                        axis=1,
+                        mode="promise_in_bounds",
+                    )
+            for v in range(g, p1):
+                own = jnp.where(lane - v * G == sub, 1.0, 0.0) if v < g + pair else 0.0
+                vs[v] = jnp.where(ingroup, own, vs[v])
+            d = spread(cols[g, 0], 0)
+            for j in range(width):
+                gv, row_at = g + j // G, j % G
+                r = 1.0 / d
+                dvec[gv] = jnp.where(sub == row_at, d, dvec[gv])
+                rvec[gv] = jnp.where(sub == row_at, r, rvec[gv])
+                us = [spread(cols[gv, c], row_at) for c in range(j + 1, width)]
+                row = spread(vs[gv], row_at)
+                if j + 1 < width:
+                    gn, next_at = g + (j + 1) // G, (j + 1) % G
+                    d = (
+                        spread(cols[gn, j + 1], next_at)
+                        - spread(cols[gn, j], next_at) * us[0] * r
+                    )
+                for v in range(gv, p1):
+                    f = cols[v, j] * r
+                    if v == gv:
+                        f = jnp.where(sub > row_at, f, 0.0)
+                    for i, c in enumerate(range(j + 1, width)):
+                        cols[v, c] = cols[v, c] - f * us[i]
+                    vs[v] = vs[v] - f * row
+        if p1 < n:
+            inside = (lane >= p0 * G) & (lane < p1 * G)
+            rows = jnp.concatenate(
+                [jnp.where(inside & (lane - g * G > sub), 0.0, vs[g]) for g in range(p0, p1)], 0
+            )
+            scaled = jnp.concatenate([vs[g] * rvec[g] for g in range(p0, p1)], 0)
+            update = dot3(scaled, rows, ((0,), (0,)))
+            for v in range(p1, n):
+                vs[v] = jnp.where(inside, 0.0, vs[v]) - update[G * v : G * v + G, :]
+    return [
+        jnp.where(lane - g * G <= sub, vs[g] * lax.rsqrt(dvec[g]), 0.0) for g in range(n)
+    ]
 
 
 def front_kernel(f_ref, map_ref, piv_ref, y_ref, first_ref, cols_ref):
@@ -192,7 +212,7 @@
 
 
 def schur_kernel(
-    fac_ref, lin_ref, v_ref, e_ref, c_ref, f_ref, s_ref, t_ref, w_ref, a_ref, sems
+    fac_ref, lin_ref, v_ref, e_ref, c_ref, f_ref, s_ref, t_ref, a_ref, w_ref, sems
 ):
     nb = 8
     copies = [None]
@@ -200,6 +220,7 @@
         part = (pl.ds(k * B, B), pl.ds(0, k * B))
         copies.append(pltpu.make_async_copy(fac_ref.at[part], a_ref.at[part], sems.at[k]))
         copies[k].start()
+    prod = None
     for k in range(nb):
         ks = slice(k * B, k * B + B)
         lc, c = k // 4, k % 4
@@ -214,10 +235,25 @@
         )
         if k:
             copies[k].wait()
-            e = e - dot3(a_ref[ks, 0 : k * B], w_ref[0 : k * B, :], ((1,), (0,)))
-        w_ref[ks, :] = dot3(lin_ref[ks, :], e, ((1,), (0,)))
-    t_ref[...] = w_ref[:, 3 * B :]
-    prod = dot3(w_ref[:, B : 3 * B], w_ref[:, 0:B], ((0,), (0,)))
+            high, low = halves(a_ref[ks, 0 : k * B])
+            left = []
+            for j in range(k):
+                js = slice(j * B, j * B + B)
+                left += [high[:, js], low[:, js], high[:, js]]
+            e = e - lax.dot_general(
+                jnp.concatenate(left, axis=1),
+                w_ref[0 : 3 * B * k, :],
+                (((1,), (0,)), ((), ())),
+                preferred_element_type=F32,
+            )
+        w = dot3(lin_ref[ks, :], e, ((1,), (0,)))
+        t_ref[ks, :] = w[:, 3 * B :]
+        if k + 1 < nb:
+            high, low = halves(w)
+            for i, x in enumerate((high, high, low)):
+                w_ref[(3 * k + i) * B : (3 * k + i + 1) * B, :] = x
+        term = dot3(w[:, B : 3 * B], w[:, 0:B], ((0,), (0,)))
+        prod = term if prod is None else prod + term
     for b in range(2):
         x = f_ref[pl.ds(2 * B * (2 + b) + 1, B, stride=2), :] - prod[b * B : b * B + B, :]
         for p in range(16):
@@ -255,7 +291,7 @@
         for i in range(len(args))
     ]
     results = [spec(pltpu.HBM if i in away_out else pltpu.VMEM) for i in range(len(outs))]
-    scratch = [pltpu.VMEM(s, F32) for s in scratch]
+    scratch = [pltpu.VMEM(s, BF16 if s[0] > 8 * B else F32) for s in scratch]
     if copies:
         scratch.append(pltpu.SemaphoreType.DMA((copies,)))
     return pl.pallas_call(
@@ -264,7 +300,7 @@
         in_specs=ins,
         out_specs=results,
         scratch_shapes=scratch,
-        compiler_params=pltpu.CompilerParams(vmem_limit_bytes=(60 if copies else 20) * 2**20),
+        compiler_params=pltpu.CompilerParams(vmem_limit_bytes=(50 if copies else 20) * 2**20),
         cost_estimate=pl.CostEstimate(
             flops=flops, bytes_accessed=8 * 2**20, transcendentals=0
         ),
@@ -302,7 +338,7 @@
     factor, inverses, coupled = kernel_call(
         chain_kernel,
         "chain",
-        [(8 * B, 8 * B), (8 * B, B), (8, B)],
+        [(32 * B, 8 * B), (8 * B, B), (8, B)],
         [(8 * B, 8 * B)],
         4 * 10**9,
         (own, other),
@@ -313,7 +349,7 @@
         schur_kernel,
         "schur",
         [(16, 2, G, B), (8 * B, B)],
-        [(8 * B, 4 * B), (8 * B, 8 * B)],
+        [(8 * B, 8 * B), (21 * B, 4 * B)],
         10**9,
         (factor, inverses, coupled, wide, cols_all, front),
         away=(0,),

time: 119 us -> 113 us (0.950)
  Pallas kernels: 44.1 us -> 38.5 us
  waiting for transfers between devices: 10.9 us -> 12.1 us
    pallas_call x4, Pallas kernels: 44.1 us -> 38.5 us  [kernel_call(): pl.pallas_call(body, out_shape=[jax.ShapeDtypeStruct(s, F32) for s in out...]
    all_to_all x1, waiting for transfers between devices: 10.9 us -> 12.1 us  [local(): lax.all_to_all(shares, 'group', split_axis=0, concat_axis=0, tiled=True)]
  transfers between devices with their start and end apart: 3 -> 3, of which waited for: 1 -> 1; matrix products, arithmetic and copies ran while one was open for 1% -> 2% of each run, Pallas kernels for 30% -> 27%
where the time goes in v4:
time: 113 us
  Pallas kernels  38.5 us (34%)
  blocking collectives  31.6 us (28%)
  starting transfers between devices  21.9 us (19%)
  waiting for transfers between devices  12.1 us (11%)
  local copies, waits for them, and re-layouts  6.62 us (6%)
  between operations  1.46 us (1%)
    pallas_call x4, Pallas kernels, kernel_call(): pl.pallas_call(body, out_shape=[jax.ShapeDtypeStruct(s, F32) for s in out...  38.5 us
    all_to_all x1, blocking collectives, local(): lax.all_to_all(jnp.broadcast_to(wide[:, :HEAD], (4, 4, HEAD, B)), 'row',...  17.8 us
    all_to_all x1, starting transfers between devices, local(): lax.all_to_all(shares, 'group', split_axis=0, concat_axis=0, tiled=True)  15 us
    all_gather x1, blocking collectives, local(): wide = lax.all_gather(first, 'col')  13.9 us
    all_to_all x1, waiting for transfers between devices, local(): lax.all_to_all(shares, 'group', split_axis=0, concat_axis=0, tiled=True)  12.1 us
    all_to_all x1, starting transfers between devices, local(): lax.all_to_all(jnp.broadcast_to(cols, (8, 2 * B, B)), 'row', split_axis=0...  5.06 us
    unnamed x18, local copies, waits for them, and re-layouts  4.87 us
  transfers between devices with their start and end apart: 3, of which 1 were waited for; matrix products, arithmetic and copies ran while one was open for 2% of the time, Pallas kernels for 27%

profile of v4, /device:TPU:2, one launch (start us, length us, event | category | flops | bytes accessed | tf_op | source)
XLA Modules:
  0.0 112.8 jit_solution(4304315871281243866)
XLA Ops:
  0.6 0.8 copy.9.map_ref
  2.0 0.0 copy-start
  2.1 1.0 copy-done
  3.1 0.0 copy-start.4
  3.1 0.7 copy-done.4
  3.8 0.8 front.1
  4.6 13.9 %all-gather = f32[1568,128]{1,0:T(8,128)S(1)} all-gather(f32[392,128]{1,0:T(8,128)S(1)} %get-tuple-element.9), channel_id=2, replica_groups=mesh['group'=16,'row'=8,'col'=4] {'col'}, dimensions={0}, use_global_device_ids=true | all-gather | bytes 1003520 | tf_op jit(solution)/shard_map/all_gather | solution.py:324
  18.5 0.1 broadcast_in_dim.24
  18.6 17.8 %all_to_all.15.own_ref = f32[4,4,136,128]{3,2,1,0:T(8,128)S(1)} all-to-all(f32[4,4,136,128]{3,2,1,0:T(8,128)S(1)} %broadcast_in_dim.24), channel_id=1, replica_groups={{0,8,16,24},{4,12,20,28},{1,9,17,25},{5,13,21,29},{2,10,18,26},{6,14,22..., dimensions={0} | all-to-all | bytes 2228224 | tf_op jit(solution)/shard_map/all_to_all | solution.py:325
  36.4 0.0 copy-start.2
  36.4 1.9 %collective-permute-start = (f32[4,4,136,128]{3,2,1,0:T(8,128)S(1)}, f32[4,4,136,128]{3,2,1,0:T(8,128)}, u32[]{:S(2)}, u32[]{:S(2)}) collective-permute-start(f32[4,4,136,128]{3,2,1,0:T(8,128)S(1)} %all_to_all.15.own_ref), channel_id=1, source_target_pairs={{0,4},{4,0},{8,12},{12,8},{16,20},{20,16},{24,28},{28,24},{1,5},{5... | collective-permute-start | bytes 3342344 | tf_op jit(solution)/shard_map/ppermute | solution.py:333
  38.3 1.0 broadcast_in_dim.25
  39.3 0.0 copy-start.6
  39.3 0.0 copy-done.2
  39.3 5.1 %all-to-all-start.1 = ((f32[8,256,128]{2,1,0:T(8,128)}), f32[8,256,128]{2,1,0:T(8,128)S(1)}, u32[]{:S(2)}, u32[]{:S(2)}) async-start(f32[8,256,128]{2,1,0:T(8,128)} %broadcast_in_dim.25), calls=%async_computation.1 | async-start | bytes 2097152 | tf_op jit(solution)/shard_map/all_to_all | solution.py:335
  44.4 0.0 copy-done.6
  44.4 0.6 gather_fusion
  45.0 0.0 copy-start.1
  45.0 0.0 collective-permute-done.other_ref
  45.0 0.0 copy-start.3
  45.1 1.3 %copy-done.3 = f32[4,4,136,128]{3,2,1,0:T(8,128)S(1)} copy-done((f32[4,4,136,128]{3,2,1,0:T(8,128)S(1)}, f32[4,4,136,128]{3,2,1,0:T(8,128)}, u32[]{:S(2)}) %copy-start.3) | copy-done | bytes 1114136
  46.4 27.7 %chain.1 = (f32[4096,1024]{1,0:T(8,128)}, f32[1024,128]{1,0:T(8,128)S(1)}, f32[8,128]{1,0:T(8,128)S(1)}) custom-call(f32[4,4,136,128]{3,2,1,0:T(8,128)S(1)} %copy-done.3, f32[4,4,136,128]{3,2,1,0:T(8,128)} %collective-permute-done.other_ref), custom_call_target="tpu_custom_call" | custom-call | flops 4000000000 | bytes 8388608 | tf_op jit(solution)/shard_map/chain/pallas_call | solution.py:297
  74.0 0.0 all-to-all-done.1.c_ref
  74.0 0.0 copy-done.1
  74.0 0.0 copy-start.5
  74.0 7.5 %schur.1 = (f32[16,2,8,128]{3,2,1,0:T(8,128)}, f32[1024,128]{1,0:T(8,128)S(1)}) custom-call(f32[4096,1024]{1,0:T(8,128)} %get-tuple-element.10.fac_ref, f32[1024,128]{1,0:T(8,128)S(1)} %get-tuple-element.11.lin_ref, f32[8,128]{1,0:T(8,128)S(1)} %get-tuple-element.12.v_ref, f32[4,392,128]{2,1,0:T(8,128)S(1)} %bitcast.32, ...), custom_call_target="tpu_custom_call" | custom-call | flops 1000000000 | bytes 8388608 | tf_op jit(solution)/shard_map/schur/pallas_call | solution.py:297
  81.6 15.0 %all-to-all-start.2 = ((f32[16,2,8,128]{3,2,1,0:T(8,128)}), f32[16,2,8,128]{3,2,1,0:T(8,128)S(1)}, u32[]{:S(2)}, u32[]{:S(2)}) async-start(f32[16,2,8,128]{3,2,1,0:T(8,128)} %get-tuple-element.14), calls=%async_computation.2 | async-start | bytes 262144 | tf_op jit(solution)/shard_map/all_to_all | solution.py:358
  96.5 0.1 and_select_fusion.1
  96.6 0.0 copy-done.5
  96.6 0.0 copy-start.7
  96.6 2.5 %sample.1 = f32[1,1024]{1,0:T(1,128)} custom-call(f32[4096,1024]{1,0:T(8,128)} %get-tuple-element.10.fac_ref, f32[1024,128]{1,0:T(8,128)S(1)} %get-tuple-element.11.lin_ref, f32[1024,128]{1,0:T(8,128)S(1)} %get-tuple-element.15.t_ref, f32[1,1024]{1,0:T(1,128)S(1)} %copy-done.5), custom_call_target="tpu_custom_call" | custom-call | flops 1000000000 | bytes 8388608 | tf_op jit(solution)/shard_map/sample/pallas_call | solution.py:297
  99.2 12.1 %all-to-all-done.2 = f32[16,2,8,128]{3,2,1,0:T(8,128)S(1)} async-done(((f32[16,2,8,128]{3,2,1,0:T(8,128)}), f32[16,2,8,128]{3,2,1,0:T(8,128)S(1)}, u32[]{:S(2)}, u32[]{:S(2)}) %all-to-all-start.2) | async-done | bytes 131104 | tf_op jit(solution)/shard_map/all_to_all | solution.py:358
  111.3 0.0 copy-done.7
  111.3 0.5 fusion.1
  111.8 1.0 copy.11
  (7 shorter events, 0.1 us)
Async XLA Ops:
  2.0 1.0 copy-start
  3.1 0.7 copy-start.4
  36.4 3.0 %copy-start.2 = (f32[4,4,136,128]{3,2,1,0:T(8,128)}, f32[4,4,136,128]{3,2,1,0:T(8,128)S(1)}, u32[]{:S(2)}) copy-start(f32[4,4,136,128]{3,2,1,0:T(8,128)S(1)} %all_to_all.15.own_ref) | copy-start | bytes 3342340
  36.4 8.7 %collective-permute-start = (f32[4,4,136,128]{3,2,1,0:T(8,128)S(1)}, f32[4,4,136,128]{3,2,1,0:T(8,128)}, u32[]{:S(2)}, u32[]{:S(2)}) collective-permute-start(f32[4,4,136,128]{3,2,1,0:T(8,128)S(1)} %all_to_all.15.own_ref), channel_id=1, source_target_pairs={{0,4},{4,0},{8,12},{12,8},{16,20},{20,16},{24,28},{28,24},{1,5},{5... | collective-permute-start | bytes 3342344 | tf_op jit(solution)/shard_map/ppermute | solution.py:333
  39.3 5.1 %copy-start.6 = (s32[16,8]{0,1:T(8,128)S(1)}, s32[16,8]{0,1:T(8,128)}, u32[]{:S(2)}) copy-start(s32[16,8]{0,1:T(8,128)} %param.8) | copy-start | bytes 1540
  39.3 34.7 %all-to-all-start.1 = ((f32[8,256,128]{2,1,0:T(8,128)}), f32[8,256,128]{2,1,0:T(8,128)S(1)}, u32[]{:S(2)}, u32[]{:S(2)}) async-start(f32[8,256,128]{2,1,0:T(8,128)} %broadcast_in_dim.25), calls=%async_computation.1 | async-start | bytes 2097152 | tf_op jit(solution)/shard_map/all_to_all | solution.py:335
  45.0 29.0 %copy-start.1 = (f32[1,4,1,128,2,1,128]{6,5,4,3,2,1,0:T(1,128)S(1)}, f32[1,4,1,128,2,1,128]{6,5,4,3,2,1,0:T(1,128)}, u32[]{:S(2)}) copy-start(f32[1,4,1,128,2,1,128]{6,5,4,3,2,1,0:T(1,128)} %param.6) | copy-start | bytes 1572868
  45.0 1.3 %copy-start.3 = (f32[4,4,136,128]{3,2,1,0:T(8,128)S(1)}, f32[4,4,136,128]{3,2,1,0:T(8,128)}, u32[]{:S(2)}) copy-start(f32[4,4,136,128]{3,2,1,0:T(8,128)} %copy-done.2) | copy-start | bytes 3342340
  74.0 22.6 %copy-start.5 = (f32[1,1024]{1,0:T(1,128)S(1)}, f32[1,1024]{1,0:T(1,128)}, u32[]{:S(2)}) copy-start(f32[1,1024]{1,0:T(1,128)} %n_ref.1) | copy-start | bytes 12292
  81.6 29.7 %all-to-all-start.2 = ((f32[16,2,8,128]{3,2,1,0:T(8,128)}), f32[16,2,8,128]{3,2,1,0:T(8,128)S(1)}, u32[]{:S(2)}, u32[]{:S(2)}) async-start(f32[16,2,8,128]{3,2,1,0:T(8,128)} %get-tuple-element.14), calls=%async_computation.2 | async-start | bytes 262144 | tf_op jit(solution)/shard_map/all_to_all | solution.py:358
  96.6 14.7 %copy-start.7 = (f32[12,1,1,8,6,1,128]{6,5,4,3,2,1,0:T(1,128)S(1)}, f32[12,1,1,8,6,1,128]{6,5,4,3,2,1,0:T(1,128)}, u32[]{:S(2)}) copy-start(f32[12,1,1,8,6,1,128]{6,5,4,3,2,1,0:T(1,128)} %param.7) | copy-start | bytes 884740

commit v5 on v4

--- a/solution.py
+++ b/solution.py
@@ -128,7 +128,7 @@
     first_ref[B : B + 1, :] = jnp.sum(
         jnp.where(i_id == t_id, sent, 0.0), axis=0, keepdims=True
     )
-    known = y_ref[pl.ds(map_ref[my_group, my_row], 1), :]
+    known = y_ref[pl.ds(map_ref[my_row, my_group], 1), :]
     for lc in range(2):
         x = block(lc, 1)
         first_ref[HEAD + lc * B : HEAD + lc * B + B, :] = x
@@ -226,33 +226,32 @@
         lc, c = k // 4, k % 4
         e = jnp.concatenate(
             [
-                e_ref[c, HEAD + lc * B : HEAD + lc * B + B, :],
-                c_ref[k, 0:B, :].T,
-                c_ref[k, B : 2 * B, :].T,
-                jnp.broadcast_to(v_ref[k : k + 1, :], (B, B)).T,
+                e_ref[c, HEAD + lc * B : HEAD + lc * B + B, :].T,
+                c_ref[k, :, :],
+                jnp.broadcast_to(v_ref[k : k + 1, :], (16, B)),
             ],
-            axis=1,
+            axis=0,
         )
         if k:
             copies[k].wait()
             high, low = halves(a_ref[ks, 0 : k * B])
-            left = []
+            right = []
             for j in range(k):
                 js = slice(j * B, j * B + B)
-                left += [high[:, js], low[:, js], high[:, js]]
+                right += [high[:, js], low[:, js], high[:, js]]
             e = e - lax.dot_general(
-                jnp.concatenate(left, axis=1),
-                w_ref[0 : 3 * B * k, :],
-                (((1,), (0,)), ((), ())),
+                w_ref[:, 0 : 3 * B * k],
+                jnp.concatenate(right, axis=1),
+                (((1,), (1,)), ((), ())),
                 preferred_element_type=F32,
             )
-        w = dot3(lin_ref[ks, :], e, ((1,), (0,)))
-        t_ref[ks, :] = w[:, 3 * B :]
+        w = dot3(e, lin_ref[ks, :], ((1,), (1,)))
+        t_ref[k : k + 1, :] = w[3 * B : 3 * B + 1, :]
         if k + 1 < nb:
             high, low = halves(w)
             for i, x in enumerate((high, high, low)):
-                w_ref[(3 * k + i) * B : (3 * k + i + 1) * B, :] = x
-        term = dot3(w[:, B : 3 * B], w[:, 0:B], ((0,), (0,)))
+                w_ref[:, (3 * k + i) * B : (3 * k + i + 1) * B] = x
+        term = dot3(w[B : 3 * B, :], w[0:B, :], ((1,), (1,)))
         prod = term if prod is None else prod + term
     for b in range(2):
         x = f_ref[pl.ds(2 * B * (2 + b) + 1, B, stride=2), :] - prod[b * B : b * B + B, :]
@@ -270,7 +269,7 @@
     xs = [None] * nb
     for k in reversed(range(nb)):
         ks = slice(k * B, k * B + B)
-        z = jnp.broadcast_to(n_ref[:, ks], (B, B)).T - t_ref[ks, :]
+        z = jnp.broadcast_to(n_ref[:, ks] - t_ref[k : k + 1, :], (B, B)).T
         if k + 1 < nb:
             copies[k].wait()
             acc = None
@@ -291,7 +290,7 @@
         for i in range(len(args))
     ]
     results = [spec(pltpu.HBM if i in away_out else pltpu.VMEM) for i in range(len(outs))]
-    scratch = [pltpu.VMEM(s, BF16 if s[0] > 8 * B else F32) for s in scratch]
+    scratch = [pltpu.VMEM(s, BF16 if s[1] > 8 * B else F32) for s in scratch]
     if copies:
         scratch.append(pltpu.SemaphoreType.DMA((copies,)))
     return pl.pallas_call(
@@ -318,7 +317,7 @@
         [(HEAD + 2 * B, B), (2 * B, B)],
         [],
         10**8,
-        (front, block_map, pivots, top_sample.reshape(-1, B)),
+        (front, block_map.T, pivots, top_sample.reshape(-1, B)),
         (1, 2),
     )
     wide = lax.all_gather(first, "col")
@@ -348,8 +347,8 @@
     shares, reduced = kernel_call(
         schur_kernel,
         "schur",
-        [(16, 2, G, B), (8 * B, B)],
-        [(8 * B, 8 * B), (21 * B, 4 * B)],
+        [(16, 2, G, B), (8, B)],
+        [(8 * B, 8 * B), (3 * B + 16, 21 * B)],
         10**9,
         (factor, inverses, coupled, wide, cols_all, front),
         away=(0,),

time: 113 us -> 115 us (1.018)
  Pallas kernels: 38.5 us -> 41.3 us
  local copies, waits for them, and re-layouts: 6.62 us -> 5.26 us
    pallas_call x4, Pallas kernels: 38.5 us -> 41.3 us  [kernel_call(): pl.pallas_call(body, out_shape=[jax.ShapeDtypeStruct(s, F32) for s in out...]
    unnamed x18 -> x15, local copies, waits for them, and re-layouts: 4.87 us -> 3.5 us
where the time goes in v5:
time: 115 us; the launch traced here: 114 us
  Pallas kernels  41.3 us (36%)
  blocking collectives  32.4 us (28%)
  starting transfers between devices  21.3 us (19%)
  waiting for transfers between devices  12.1 us (11%)
  local copies, waits for them, and re-layouts  5.26 us (5%)
  between operations  1.44 us (1%)
    pallas_call x4, Pallas kernels, kernel_call(): pl.pallas_call(body, out_shape=[jax.ShapeDtypeStruct(s, F32) for s in out...  41.3 us
    all_to_all x1, blocking collectives, local(): lax.all_to_all(jnp.broadcast_to(wide[:, :HEAD], (4, 4, HEAD, B)), 'row',...  18.5 us
    all_to_all x1, starting transfers between devices, local(): lax.all_to_all(shares, 'group', split_axis=0, concat_axis=0, tiled=True)  14.3 us
    all_gather x1, blocking collectives, local(): wide = lax.all_gather(first, 'col')  13.9 us
    all_to_all x1, waiting for transfers between devices, local(): lax.all_to_all(shares, 'group', split_axis=0, concat_axis=0, tiled=True)  12.1 us
    all_to_all x1, starting transfers between devices, local(): lax.all_to_all(jnp.broadcast_to(cols, (8, 2 * B, B)), 'row', split_axis=0...  5.06 us
    unnamed x15, local copies, waits for them, and re-layouts  3.5 us
  transfers between devices with their start and end apart: 3, of which 1 were waited for; matrix products, arithmetic and copies ran while one was open for 2% of the time, Pallas kernels for 27%

profile of v5, /device:TPU:2, one launch (start us, length us, event | category | flops | bytes accessed | tf_op | source)
XLA Modules:
  0.0 114.4 jit_solution(65924900778341095)
XLA Ops:
  1.3 0.0 copy-start
  1.3 1.0 copy-done
  2.3 0.0 copy-start.2
  2.3 0.7 copy-done.2
  3.0 0.0 copy-start.4
  3.0 0.7 copy-done.4
  3.7 0.7 front.1
  4.5 13.9 %all-gather = f32[1568,128]{1,0:T(8,128)S(1)} all-gather(f32[392,128]{1,0:T(8,128)S(1)} %get-tuple-element.9), channel_id=2, replica_groups=mesh['group'=16,'row'=8,'col'=4] {'col'}, dimensions={0}, use_global_device_ids=true | all-gather | bytes 1003520 | tf_op jit(solution)/shard_map/all_gather | solution.py:323
  18.4 0.1 broadcast_in_dim.24
  18.4 18.5 %all_to_all.15.own_ref = f32[4,4,136,128]{3,2,1,0:T(8,128)} all-to-all(f32[4,4,136,128]{3,2,1,0:T(8,128)S(1)} %broadcast_in_dim.24), channel_id=1, replica_groups={{0,8,16,24},{4,12,20,28},{1,9,17,25},{5,13,21,29},{2,10,18,26},{6,14,22..., dimensions={0} | all-to-all | bytes 2228224 | tf_op jit(solution)/shard_map/all_to_all | solution.py:324
  37.0 1.9 %collective-permute-start = (f32[4,4,136,128]{3,2,1,0:T(8,128)}, f32[4,4,136,128]{3,2,1,0:T(8,128)}, u32[]{:S(2)}, u32[]{:S(2)}) collective-permute-start(f32[4,4,136,128]{3,2,1,0:T(8,128)} %all_to_all.15.own_ref), channel_id=1, source_target_pairs={{0,4},{4,0},{8,12},{12,8},{16,20},{20,16},{24,28},{28,24},{1,5},{5... | collective-permute-start | bytes 3342344 | tf_op jit(solution)/shard_map/ppermute | solution.py:332
  38.9 1.1 broadcast_in_dim.25
  39.9 0.0 copy-start.3
  39.9 5.1 %all-to-all-start.1 = ((f32[8,256,128]{2,1,0:T(8,128)}), f32[8,256,128]{2,1,0:T(8,128)S(1)}, u32[]{:S(2)}, u32[]{:S(2)}) async-start(f32[8,256,128]{2,1,0:T(8,128)} %broadcast_in_dim.25), calls=%async_computation.1 | async-start | bytes 2097152 | tf_op jit(solution)/shard_map/all_to_all | solution.py:334
  45.0 0.0 copy-done.3
  45.0 0.6 gather_fusion
  45.6 0.0 copy-start.1
  45.6 0.0 collective-permute-done.other_ref
  45.6 28.0 %chain.1 = (f32[4096,1024]{1,0:T(8,128)}, f32[1024,128]{1,0:T(8,128)S(1)}, f32[8,128]{1,0:T(8,128)S(1)}) custom-call(f32[4,4,136,128]{3,2,1,0:T(8,128)} %all_to_all.15.own_ref, f32[4,4,136,128]{3,2,1,0:T(8,128)} %collective-permute-done.other_ref), custom_call_target="tpu_custom_call" | custom-call | flops 4000000000 | bytes 8388608 | tf_op jit(solution)/shard_map/chain/pallas_call | solution.py:296
  73.7 0.0 all-to-all-done.1.c_ref
  73.7 0.0 copy-done.1
  73.7 0.0 copy-start.5
  73.7 10.0 %schur.1 = (f32[16,2,8,128]{3,2,1,0:T(8,128)}, f32[8,128]{1,0:T(8,128)S(1)}) custom-call(f32[4096,1024]{1,0:T(8,128)} %get-tuple-element.10.fac_ref, f32[1024,128]{1,0:T(8,128)S(1)} %get-tuple-element.11.lin_ref, f32[8,128]{1,0:T(8,128)S(1)} %get-tuple-element.12.v_ref, f32[4,392,128]{2,1,0:T(8,128)S(1)} %bitcast.33, ...), custom_call_target="tpu_custom_call" | custom-call | flops 1000000000 | bytes 8388608 | tf_op jit(solution)/shard_map/schur/pallas_call | solution.py:296
  83.7 14.3 %all-to-all-start.2 = ((f32[16,2,8,128]{3,2,1,0:T(8,128)}), f32[16,2,8,128]{3,2,1,0:T(8,128)S(1)}, u32[]{:S(2)}, u32[]{:S(2)}) async-start(f32[16,2,8,128]{3,2,1,0:T(8,128)} %get-tuple-element.14), calls=%async_computation.2 | async-start | bytes 262144 | tf_op jit(solution)/shard_map/all_to_all | solution.py:357
  98.1 0.1 and_select_fusion.1
  98.2 0.0 copy-done.5
  98.2 0.0 copy-start.6
  98.2 2.5 %sample.1 = f32[1,1024]{1,0:T(1,128)} custom-call(f32[4096,1024]{1,0:T(8,128)} %get-tuple-element.10.fac_ref, f32[1024,128]{1,0:T(8,128)S(1)} %get-tuple-element.11.lin_ref, f32[8,128]{1,0:T(8,128)S(1)} %get-tuple-element.15.t_ref, f32[1,1024]{1,0:T(1,128)S(1)} %copy-done.5), custom_call_target="tpu_custom_call" | custom-call | flops 1000000000 | bytes 8388608 | tf_op jit(solution)/shard_map/sample/pallas_call | solution.py:296
  100.7 12.1 %all-to-all-done.2 = f32[16,2,8,128]{3,2,1,0:T(8,128)S(1)} async-done(((f32[16,2,8,128]{3,2,1,0:T(8,128)}), f32[16,2,8,128]{3,2,1,0:T(8,128)S(1)}, u32[]{:S(2)}, u32[]{:S(2)}) %all-to-all-start.2) | async-done | bytes 131104 | tf_op jit(solution)/shard_map/all_to_all | solution.py:357
  112.8 0.0 copy-done.6
  112.8 0.5 fusion.1
  113.4 1.0 copy.10
  (7 shorter events, 0.1 us)
Async XLA Ops:
  1.3 1.0 copy-start
  2.3 0.7 copy-start.2
  3.0 0.7 copy-start.4
  37.0 8.7 %collective-permute-start = (f32[4,4,136,128]{3,2,1,0:T(8,128)}, f32[4,4,136,128]{3,2,1,0:T(8,128)}, u32[]{:S(2)}, u32[]{:S(2)}) collective-permute-start(f32[4,4,136,128]{3,2,1,0:T(8,128)} %all_to_all.15.own_ref), channel_id=1, source_target_pairs={{0,4},{4,0},{8,12},{12,8},{16,20},{20,16},{24,28},{28,24},{1,5},{5... | collective-permute-start | bytes 3342344 | tf_op jit(solution)/shard_map/ppermute | solution.py:332
  39.9 5.1 %copy-start.3 = (s32[16,8]{0,1:T(8,128)S(1)}, s32[16,8]{0,1:T(8,128)}, u32[]{:S(2)}) copy-start(s32[16,8]{0,1:T(8,128)} %param.8) | copy-start | bytes 1540
  39.9 33.7 %all-to-all-start.1 = ((f32[8,256,128]{2,1,0:T(8,128)}), f32[8,256,128]{2,1,0:T(8,128)S(1)}, u32[]{:S(2)}, u32[]{:S(2)}) async-start(f32[8,256,128]{2,1,0:T(8,128)} %broadcast_in_dim.25), calls=%async_computation.1 | async-start | bytes 2097152 | tf_op jit(solution)/shard_map/all_to_all | solution.py:334
  45.6 28.1 %copy-start.1 = (f32[1,4,1,128,2,1,128]{6,5,4,3,2,1,0:T(1,128)S(1)}, f32[1,4,1,128,2,1,128]{6,5,4,3,2,1,0:T(1,128)}, u32[]{:S(2)}) copy-start(f32[1,4,1,128,2,1,128]{6,5,4,3,2,1,0:T(1,128)} %param.6) | copy-start | bytes 1572868
  73.7 24.5 %copy-start.5 = (f32[1,1024]{1,0:T(1,128)S(1)}, f32[1,1024]{1,0:T(1,128)}, u32[]{:S(2)}) copy-start(f32[1,1024]{1,0:T(1,128)} %n_ref.1) | copy-start | bytes 12292
  83.7 29.0 %all-to-all-start.2 = ((f32[16,2,8,128]{3,2,1,0:T(8,128)}), f32[16,2,8,128]{3,2,1,0:T(8,128)S(1)}, u32[]{:S(2)}, u32[]{:S(2)}) async-start(f32[16,2,8,128]{3,2,1,0:T(8,128)} %get-tuple-element.14), calls=%async_computation.2 | async-start | bytes 262144 | tf_op jit(solution)/shard_map/all_to_all | solution.py:357
  98.2 14.7 %copy-start.6 = (f32[12,1,1,8,6,1,128]{6,5,4,3,2,1,0:T(1,128)S(1)}, f32[12,1,1,8,6,1,128]{6,5,4,3,2,1,0:T(1,128)}, u32[]{:S(2)}) copy-start(f32[12,1,1,8,6,1,128]{6,5,4,3,2,1,0:T(1,128)} %param.7) | copy-start | bytes 884740

commit v6 on v4

--- a/solution.py
+++ b/solution.py
@@ -282,6 +282,18 @@
         x_ref[:, ks] = xs[k]
 
 
+def place_kernel(map_ref, top_ref, got_ref, out_ref):
+    my_row = lax.axis_index("row")
+    my_col = lax.axis_index("col")
+    out_ref[...] = top_ref[...]
+    for g in range(16):
+        row = map_ref[g, my_row] >> 3
+        for b in range(2):
+            col = map_ref[g, 4 * b + my_col] >> 2
+            rows = pl.ds(col * (6 * G) + row, G, stride=6)
+            out_ref[rows, :] = out_ref[rows, :] + got_ref[g, b, :, :]
+
+
 def kernel_call(body, name, outs, scratch, flops, args, smem=(), away=(), away_out=(), copies=0):
     def spec(space):
         return pl.BlockSpec(memory_space=space)
@@ -309,8 +321,6 @@
 
 
 def local(child_front, top_front, block_map, pivots, noise, top_sample):
-    my_row = lax.axis_index("row")
-    my_col = lax.axis_index("col")
     front = child_front.reshape(8 * B, B)
     first, cols = kernel_call(
         front_kernel,
@@ -367,21 +377,16 @@
         copies=8,
     )
 
-    col_blocks = jnp.arange(2, dtype=jnp.int32) * 4 + my_col
-    col_target = jnp.take(block_map, col_blocks, axis=1) // 4
-    row_target = lax.dynamic_index_in_dim(block_map, my_row, 1, keepdims=False) // 8
-    top_cols = top_front.shape[0]
-    top_rows = top_front.shape[4]
-    col_hot = (
-        col_target[:, :, None] == jnp.arange(top_cols, dtype=jnp.int32)[None, None, :]
-    ).astype(F32)
-    row_hot = (
-        row_target[:, None] == jnp.arange(top_rows, dtype=jnp.int32)[None, :]
-    ).astype(F32)
-    top_tile = top_front.reshape(top_cols, G, top_rows, B)
-    placed = row_hot[:, None, None, :, None] * arrived[:, :, :, None, :]
-    top_tile = top_tile + jnp.einsum("gak,gamli->kmli", col_hot, placed, precision=HIGH)
-    return (top_tile.reshape(top_front.shape), solved)
+    (top_out,) = kernel_call(
+        place_kernel,
+        "place",
+        [(12 * 6 * G, B)],
+        [],
+        10**6,
+        (block_map, top_front.reshape(12 * 6 * G, B), arrived),
+        (0,),
+    )
+    return (top_out.reshape(top_front.shape), solved)
 
 
 def solution(mesh):

time: 113 us -> 113 us (level)
  local copies, waits for them, and re-layouts: 6.62 us -> 5.01 us
  Pallas kernels: 38.5 us -> 40.1 us
    pallas_call x4 -> x5, Pallas kernels: 38.5 us -> 40.1 us  [kernel_call(): pl.pallas_call(body, out_shape=[jax.ShapeDtypeStruct(s, F32) for s in out...]
    unnamed x18 -> x15, local copies, waits for them, and re-layouts: 4.87 us -> 3.85 us
  transfers between devices with their start and end apart: 3 -> 3, of which waited for: 1 -> 1; matrix products, arithmetic and copies ran while one was open for 2% -> 1% of each run, Pallas kernels for 27% -> 27%
where the time goes in v6:
time: 113 us; the launch traced here: 112 us
  Pallas kernels  40.1 us (35%)
  blocking collectives  31.6 us (28%)
  starting transfers between devices  21.8 us (19%)
  waiting for transfers between devices  12.1 us (11%)
  local copies, waits for them, and re-layouts  5.01 us (4%)
  between operations  1.4 us (1%)
    pallas_call x5, Pallas kernels, kernel_call(): pl.pallas_call(body, out_shape=[jax.ShapeDtypeStruct(s, F32) for s in out...  40.1 us
    all_to_all x1, blocking collectives, local(): lax.all_to_all(jnp.broadcast_to(wide[:, :HEAD], (4, 4, HEAD, B)), 'row',...  17.8 us
    all_to_all x1, starting transfers between devices, local(): lax.all_to_all(shares, 'group', split_axis=0, concat_axis=0, tiled=True)  15 us
    all_gather x1, blocking collectives, local(): wide = lax.all_gather(first, 'col')  13.9 us
    all_to_all x1, waiting for transfers between devices, local(): lax.all_to_all(shares, 'group', split_axis=0, concat_axis=0, tiled=True)  12.1 us
    all_to_all x1, starting transfers between devices, local(): lax.all_to_all(jnp.broadcast_to(cols, (8, 2 * B, B)), 'row', split_axis=0...  4.92 us
    unnamed x15, local copies, waits for them, and re-layouts  3.85 us
  transfers between devices with their start and end apart: 3, of which 1 were waited for; matrix products, arithmetic and copies ran while one was open for 1% of the time, Pallas kernels for 27%

profile of v6, /device:TPU:2, one launch (start us, length us, event | category | flops | bytes accessed | tf_op | source)
XLA Modules:
  0.0 112.1 jit_solution(16910918542532414623)
XLA Ops:
  0.6 0.8 copy.12.map_ref
  2.0 0.0 copy-start
  2.1 1.0 copy-done
  3.1 0.0 copy-start.5
  3.1 0.7 copy-done.5
  3.8 0.8 front.1
  4.6 13.9 %all-gather = f32[1568,128]{1,0:T(8,128)S(1)} all-gather(f32[392,128]{1,0:T(8,128)S(1)} %get-tuple-element.9), channel_id=2, replica_groups=mesh['group'=16,'row'=8,'col'=4] {'col'}, dimensions={0}, use_global_device_ids=true | all-gather | bytes 1003520 | tf_op jit(solution)/shard_map/all_gather | solution.py:334
  18.5 0.1 broadcast_in_dim.6
  18.6 17.8 %all_to_all.15.own_ref = f32[4,4,136,128]{3,2,1,0:T(8,128)S(1)} all-to-all(f32[4,4,136,128]{3,2,1,0:T(8,128)S(1)} %broadcast_in_dim.6), channel_id=1, replica_groups={{0,8,16,24},{4,12,20,28},{1,9,17,25},{5,13,21,29},{2,10,18,26},{6,14,22..., dimensions={0} | all-to-all | bytes 2228224 | tf_op jit(solution)/shard_map/all_to_all | solution.py:335
  36.4 0.0 copy-start.2
  36.4 1.9 %collective-permute-start = (f32[4,4,136,128]{3,2,1,0:T(8,128)S(1)}, f32[4,4,136,128]{3,2,1,0:T(8,128)}, u32[]{:S(2)}, u32[]{:S(2)}) collective-permute-start(f32[4,4,136,128]{3,2,1,0:T(8,128)S(1)} %all_to_all.15.own_ref), channel_id=1, source_target_pairs={{0,4},{4,0},{8,12},{12,8},{16,20},{20,16},{24,28},{28,24},{1,5},{5... | collective-permute-start | bytes 3342344 | tf_op jit(solution)/shard_map/ppermute | solution.py:343
  38.3 1.1 broadcast_in_dim.7
  39.4 0.0 copy-done.2
  39.4 4.9 %all-to-all-start.1 = ((f32[8,256,128]{2,1,0:T(8,128)}), f32[8,256,128]{2,1,0:T(8,128)S(1)}, u32[]{:S(2)}, u32[]{:S(2)}) async-start(f32[8,256,128]{2,1,0:T(8,128)} %broadcast_in_dim.7), calls=%async_computation.1 | async-start | bytes 2097152 | tf_op jit(solution)/shard_map/all_to_all | solution.py:345
  44.3 0.0 copy-start.1
  44.3 0.0 collective-permute-done.other_ref
  44.3 0.0 copy-start.3
  44.3 1.3 %copy-done.3 = f32[4,4,136,128]{3,2,1,0:T(8,128)S(1)} copy-done((f32[4,4,136,128]{3,2,1,0:T(8,128)S(1)}, f32[4,4,136,128]{3,2,1,0:T(8,128)}, u32[]{:S(2)}) %copy-start.3) | copy-done | bytes 1114136
  45.6 27.7 %chain.1 = (f32[4096,1024]{1,0:T(8,128)}, f32[1024,128]{1,0:T(8,128)S(1)}, f32[8,128]{1,0:T(8,128)S(1)}) custom-call(f32[4,4,136,128]{3,2,1,0:T(8,128)S(1)} %copy-done.3, f32[4,4,136,128]{3,2,1,0:T(8,128)} %collective-permute-done.other_ref), custom_call_target="tpu_custom_call" | custom-call | flops 4000000000 | bytes 8388608 | tf_op jit(solution)/shard_map/chain/pallas_call | solution.py:309
  73.3 0.0 all-to-all-done.1.c_ref
  73.3 0.0 copy-done.1
  73.3 0.0 copy-start.6
  73.4 7.5 %schur.1 = (f32[16,2,8,128]{3,2,1,0:T(8,128)}, f32[1024,128]{1,0:T(8,128)S(1)}) custom-call(f32[4096,1024]{1,0:T(8,128)} %get-tuple-element.10.fac_ref, f32[1024,128]{1,0:T(8,128)S(1)} %get-tuple-element.11.lin_ref, f32[8,128]{1,0:T(8,128)S(1)} %get-tuple-element.12.v_ref, f32[4,392,128]{2,1,0:T(8,128)S(1)} %bitcast.6, ...), custom_call_target="tpu_custom_call" | custom-call | flops 1000000000 | bytes 8388608 | tf_op jit(solution)/shard_map/schur/pallas_call | solution.py:309
  80.9 15.0 %all-to-all-start.2 = ((f32[16,2,8,128]{3,2,1,0:T(8,128)}), f32[16,2,8,128]{3,2,1,0:T(8,128)S(1)}, u32[]{:S(2)}, u32[]{:S(2)}) async-start(f32[16,2,8,128]{3,2,1,0:T(8,128)} %get-tuple-element.14), calls=%async_computation.2 | async-start | bytes 262144 | tf_op jit(solution)/shard_map/all_to_all | solution.py:368
  95.8 0.0 copy-done.6
  95.8 0.0 copy-start.4
  95.9 2.5 %sample.1 = f32[1,1024]{1,0:T(1,128)} custom-call(f32[4096,1024]{1,0:T(8,128)} %get-tuple-element.10.fac_ref, f32[1024,128]{1,0:T(8,128)S(1)} %get-tuple-element.11.lin_ref, f32[1024,128]{1,0:T(8,128)S(1)} %get-tuple-element.15.t_ref, f32[1,1024]{1,0:T(1,128)S(1)} %copy-done.6), custom_call_target="tpu_custom_call" | custom-call | flops 1000000000 | bytes 8388608 | tf_op jit(solution)/shard_map/sample/pallas_call | solution.py:309
  98.4 12.1 %all-to-all-done.2.got_ref = f32[16,2,8,128]{3,2,1,0:T(8,128)S(1)} async-done(((f32[16,2,8,128]{3,2,1,0:T(8,128)}), f32[16,2,8,128]{3,2,1,0:T(8,128)S(1)}, u32[]{:S(2)}, u32[]{:S(2)}) %all-to-all-start.2) | async-done | bytes 131104 | tf_op jit(solution)/shard_map/all_to_all | solution.py:368
  110.5 0.0 copy-done.4
  110.5 1.5 %place.1 = f32[576,128]{1,0:T(8,128)} custom-call(s32[16,8]{1,0:T(8,128)S(1)} %copy.12.map_ref, f32[576,128]{1,0:T(8,128)S(1)} %bitcast.9, f32[16,2,8,128]{3,2,1,0:T(8,128)S(1)} %all-to-all-done.2.got_ref), custom_call_target="tpu_custom_call" | custom-call | flops 1000000 | bytes 8388608 | tf_op jit(solution)/shard_map/place/pallas_call | solution.py:309
  (1 shorter events, 0.0 us)
Async XLA Ops:
  2.0 1.0 copy-start
  3.1 0.7 copy-start.5
  36.4 3.0 %copy-start.2 = (f32[4,4,136,128]{3,2,1,0:T(8,128)}, f32[4,4,136,128]{3,2,1,0:T(8,128)S(1)}, u32[]{:S(2)}) copy-start(f32[4,4,136,128]{3,2,1,0:T(8,128)S(1)} %all_to_all.15.own_ref) | copy-start | bytes 3342340
  36.4 7.9 %collective-permute-start = (f32[4,4,136,128]{3,2,1,0:T(8,128)S(1)}, f32[4,4,136,128]{3,2,1,0:T(8,128)}, u32[]{:S(2)}, u32[]{:S(2)}) collective-permute-start(f32[4,4,136,128]{3,2,1,0:T(8,128)S(1)} %all_to_all.15.own_ref), channel_id=1, source_target_pairs={{0,4},{4,0},{8,12},{12,8},{16,20},{20,16},{24,28},{28,24},{1,5},{5... | collective-permute-start | bytes 3342344 | tf_op jit(solution)/shard_map/ppermute | solution.py:343
  39.4 34.0 %all-to-all-start.1 = ((f32[8,256,128]{2,1,0:T(8,128)}), f32[8,256,128]{2,1,0:T(8,128)S(1)}, u32[]{:S(2)}, u32[]{:S(2)}) async-start(f32[8,256,128]{2,1,0:T(8,128)} %broadcast_in_dim.7), calls=%async_computation.1 | async-start | bytes 2097152 | tf_op jit(solution)/shard_map/all_to_all | solution.py:345
  44.3 29.0 %copy-start.1 = (f32[1,4,1,128,2,1,128]{6,5,4,3,2,1,0:T(1,128)S(1)}, f32[1,4,1,128,2,1,128]{6,5,4,3,2,1,0:T(1,128)}, u32[]{:S(2)}) copy-start(f32[1,4,1,128,2,1,128]{6,5,4,3,2,1,0:T(1,128)} %param.6) | copy-start | bytes 1572868
  44.3 1.3 %copy-start.3 = (f32[4,4,136,128]{3,2,1,0:T(8,128)S(1)}, f32[4,4,136,128]{3,2,1,0:T(8,128)}, u32[]{:S(2)}) copy-start(f32[4,4,136,128]{3,2,1,0:T(8,128)} %copy-done.2) | copy-start | bytes 3342340
  73.3 22.5 %copy-start.6 = (f32[1,1024]{1,0:T(1,128)S(1)}, f32[1,1024]{1,0:T(1,128)}, u32[]{:S(2)}) copy-start(f32[1,1024]{1,0:T(1,128)} %n_ref.1) | copy-start | bytes 12292
  80.9 29.7 %all-to-all-start.2 = ((f32[16,2,8,128]{3,2,1,0:T(8,128)}), f32[16,2,8,128]{3,2,1,0:T(8,128)S(1)}, u32[]{:S(2)}, u32[]{:S(2)}) async-start(f32[16,2,8,128]{3,2,1,0:T(8,128)} %get-tuple-element.14), calls=%async_computation.2 | async-start | bytes 262144 | tf_op jit(solution)/shard_map/all_to_all | solution.py:368
  95.8 14.7 %copy-start.4 = (f32[12,1,1,8,6,1,128]{6,5,4,3,2,1,0:T(1,128)S(1)}, f32[12,1,1,8,6,1,128]{6,5,4,3,2,1,0:T(1,128)}, u32[]{:S(2)}) copy-start(f32[12,1,1,8,6,1,128]{6,5,4,3,2,1,0:T(1,128)} %param.7) | copy-start | bytes 884740
